TPU v7x, 256 devices: a whole 4x4x8 slice. The times are simulated.
256 devices in a mesh: gx: 8 (over x, core), gy: 8 (over z), gz: 4 (over y).
Axes of the slice: x: 4, y: 4, z: 8, core: 2. Of those that a mesh axis runs over, the one named last changes fastest.
Arguments:
- local_displacement: float32 [8, 8, 4, 6, 128, 128], P('gx', 'gy', 'gz'), may hold values from -6 to 6
- coarse_load: float32 [8, 8, 4, 6, 128], P('gx', 'gy', 'gz'), may hold values from -12 to 12
- flexibility: float32 [8, 8, 4, 768, 768], P('gx', 'gy', 'gz'), as said below
- block_map: int32 [8, 8, 4, 768], P('gx', 'gy', 'gz'), may hold values from 0 to 767, each once within a row
- mode_counts: int32 [8, 8, 4], P('gx', 'gy', 'gz'), may hold values from 3 to 6, as said below
- mode_traces: float32 [8, 8, 4, 6, 6, 128], P('gx', 'gy', 'gz')
- coarse_rows: float32 [8, 8, 4, 6, 1536], P('gx', 'gy', 'gz'), as said below
- stored_dirs: float32 [8, 8, 4, 40, 6, 128], P('gx', 'gy', 'gz'), as said below
- stored_images: float32 [8, 8, 4, 40, 6, 128], P('gx', 'gy', 'gz'), as said below
- stored_curv: float32 [40], replicated, may hold values from 1 to 4
Outputs:
- multipliers: float32 [8, 8, 4, 6, 128, 128], P('gx', 'gy', 'gz')
- residual: float32 [8, 8, 4, 6, 128, 128], P('gx', 'gy', 'gz')
Inputs may be any that keep to these rules, and one draw needn't show every extreme that they name: `flexibility`: each subdomain's matrix is symmetric positive definite. `coarse_rows`: read as a [1536, 1536] matrix it is exactly symmetric: the inverse of G^T G for the coarse basis G of the present modes, with ones added on the diagonal of absent modes. `mode_counts`: modes numbered from the count on are absent. `block_map`: each subdomain's row names every interface position once. `stored_dirs`: both copies of every face agree: slot 2a of a subdomain equals slot 2a+1 of its lower neighbour along grid dimension a. `stored_images`: both copies of every face agree: slot 2a of a subdomain equals slot 2a+1 of its lower neighbour along grid dimension a.
All inputs are finite; a program needn't handle non-finite values.
Results may differ from a plain program's by a relative error of at most 0.0003.
Values sent between devices are 32-bit elements; how exact they have to be, the bound alone decides.
A program may use at most 128 MiB of HBM per device.

v0:
```python
import functools

import jax
import jax.numpy as jnp
from jax import lax
from jax.experimental import pallas as pl
from jax.experimental.pallas import tpu as pltpu
from jax.sharding import PartitionSpec as P

F32, BF16 = jnp.float32, jnp.bfloat16
AXES = ("gx", "gy", "gz")
FACE = 128
NB = 6 * FACE
STORED = 40
STEPS = 5


def dot(a, b):
    return jnp.dot(a, b, preferred_element_type=F32)


def split(x):
    high = x.astype(BF16)
    return high, (x - high.astype(F32)).astype(BF16)


def wide(x):
    return jnp.concatenate(split(x), axis=1)


def fold(product, rows):
    half = product.shape[1] // 2
    return (product[:rows, :half] + product[:rows, half:]) + product[rows:, :half]


def thrice(x):
    high, low = split(x)
    high, low = high.astype(F32), low.astype(F32)
    return (high + pltpu.roll(low, STORED, 1) + pltpu.roll(high, 2 * STORED, 1)).astype(BF16)


def kernel(sizes, disp_hbm, load, flex_hbm, bmap, counts, traces, rows, dirs, images, curv, lam_out, res_out, s):
    nx, ny, nz = sizes
    me = dict(zip(AXES, (lax.axis_index(a) for a in AXES)))
    count = dict(zip(AXES, sizes))

    def other(axis, delta):
        return lax.rem(me[axis] + (count[axis] + delta), count[axis])

    barrier = pltpu.get_barrier_semaphore()
    for axis in AXES:
        for delta in range(1, count[axis]):
            pl.semaphore_signal(barrier, inc=1, device_id={axis: other(axis, delta)}, device_id_type=pl.DeviceIdType.MESH)

    fetch_flex = pltpu.make_async_copy(flex_hbm, s["flex"], s["local"].at[0])
    fetch_flex.start()
    fetch_disp = pltpu.make_async_copy(disp_hbm, s["disp"], s["local"].at[1])
    fetch_disp.start()

    used = [0]
    unsent = []

    def phase():
        used[0] += 1
        return s["sent"].at[used[0] - 1], s["came"].at[used[0] - 1]

    def wait_bytes(ref, sem):
        pltpu.make_async_copy(ref, ref, sem).wait()

    def send(src, dst, sems, target):
        pltpu.make_async_remote_copy(
            src_ref=src,
            dst_ref=dst,
            send_sem=sems[0],
            recv_sem=sems[1],
            device_id=target,
            device_id_type=pl.DeviceIdType.MESH,
        ).start()

    def finish(sems, ref):
        unsent.append((sems[0], ref))
        return lambda: wait_bytes(ref, sems[1])

    def to_faces(piece, dst):
        sems = phase()
        for slot in (2, 3, 4, 5, 0, 1):
            axis = AXES[slot // 2]
            target = {axis: other(axis, 1 if slot % 2 else -1)}
            send(piece(slot), dst.at[slot ^ 1], sems, target)
        return finish(sems, dst)

    def to_all(axis, src, dst):
        sems = phase()
        for delta in range(1, count[axis]):
            send(src, dst.at[me[axis]], sems, {axis: other(axis, delta)})
        return finish(sems, dst.at[pl.ds(0, count[axis] - 1)])

    def to_each(axis, src, dst):
        sems = phase()
        for delta in range(1, count[axis]):
            peer = other(axis, delta)
            send(src.at[peer], dst.at[me[axis]], sems, {axis: peer})
        return finish(sems, dst.at[pl.ds(0, count[axis] - 1)])

    def total(buf):
        out = buf[0]
        for j in range(1, buf.shape[0]):
            out = out + buf[j]
        return out

    own_rows, own_cut = s["own_rows"], s["cut"]
    own_rows[...] = jnp.zeros_like(own_rows)
    own_rows[0:6, :] = rows[...]
    group = nz * 6
    own_cut[...] = jnp.zeros_like(own_cut)
    for j in range(ny):
        for i in range(nx):
            at = (i * ny + j) * group
            own_cut[j, :, i * group : (i + 1) * group] = own_rows[:, at : at + group]

    present = lax.broadcasted_iota(jnp.int32, (6, FACE), 0) < counts[0, 0, 0]
    own_modes = s["own_modes"]
    own_modes[...] = jnp.zeros_like(own_modes)
    for slot in range(6):
        sign = 1.0 if slot % 2 else -1.0
        own_modes[slot, 0:6, :] = jnp.where(present, sign * traces[:, slot, :], 0.0)

    block = s["block0"]
    block[...] = jnp.zeros_like(block)
    block[0:6, :] = load[...]

    pl.semaphore_wait(barrier, nx + ny + nz - 3)

    def coarse_x(k, c):
        s[f"gx{k}"][me["gx"]] = c
        return to_all("gx", s[f"gx{k}"].at[me["gx"]], s[f"gx{k}"])

    def coarse_z(k):
        s[f"gz{k}"][me["gz"]] = s[f"gx{k}"][...]
        return to_all("gz", s[f"gx{k}"], s[f"gz{k}"])

    def coarse_y(k):
        width = s[f"gx{k}"].shape[-1]
        c = s[f"gz{k}"][...].reshape(nx * nz * 8, width)
        if width == FACE:
            partial = fold(dot(s["inverse"][...], wide(c)), ny * 8)
        else:
            partial = jnp.concatenate(
                [fold(dot(s["inverse"][...], wide(c[:, at : at + FACE])), ny * 8) for at in range(0, width, FACE)], axis=1
            )
        s[f"part{k}"][...] = partial.reshape(ny, 8, width)
        s[f"gy{k}"][me["gy"]] = s[f"part{k}"][me["gy"]]
        return to_each("gy", s[f"part{k}"], s[f"gy{k}"])

    def coarse_faces(k):
        s[f"alpha{k}"][...] = total(s[f"gy{k}"])
        return to_faces(lambda slot: s[f"alpha{k}"], s[f"near{k}"])

    def graph(k, slot, at=0):
        own = s[f"alpha{k}"][:, at : at + FACE]
        near = s[f"near{k}"][slot, :, at : at + FACE]
        a = jnp.concatenate([own, near], axis=0)
        high, low = split(a)
        high, low = high.astype(F32), low.astype(F32)
        stack = jnp.concatenate([high, high, low, jnp.zeros((FACE - 48, FACE), F32)], axis=0).astype(BF16)
        return dot(s["basis"][slot], stack)

    def face(ref, slot):
        return ref[slot * FACE : (slot + 1) * FACE, :]

    def modes_dot(z):
        return fold(dot(s["modes2"][...], wide(z)), 8)

    came_x = to_all("gx", block, s["gx0"])
    s["gx0"][me["gx"]] = block[...]
    came_cut = to_each("gy", own_cut, s["all_cut"])
    s["all_cut"][me["gy"]] = own_cut[me["gy"]]
    came_modes = to_faces(lambda slot: own_modes.at[slot], s["near_modes"])

    modes = jnp.concatenate([own_modes[slot] for slot in range(6)], axis=1)
    high, low = split(modes)
    s["modes2"][...] = jnp.concatenate([high.astype(F32), low.astype(F32)], axis=0).astype(BF16)

    fetch_flex.wait()

    def cut_flex(i, carry):
        at = pl.ds(pl.multiple_of(i * FACE, FACE), FACE)
        high, low = split(s["flex"][at, :])
        s["flex2"][at, 0:NB] = high
        s["flex2"][at, NB : 2 * NB] = low
        sign = lax.convert_element_type(2 * lax.rem(i, 2) - 1, F32)
        spot = i * FACE + lax.broadcasted_iota(jnp.int32, (FACE, NB), 0)
        s["pick"][at, :] = jnp.where(bmap[...] == spot, sign, 0.0).astype(BF16)
        return carry

    lax.fori_loop(0, 6, cut_flex, 0)

    def pick_rows(i, carry):
        at = pl.multiple_of(i * FACE, FACE)
        out = dot(s["pick"][pl.ds(at, FACE), :], s["flex2"][...])
        s["half"][pl.ds(at, FACE), :] = out[:, 0:NB].astype(BF16)
        s["half"][pl.ds(NB + at, FACE), :] = out[:, NB : 2 * NB].astype(BF16)
        return carry

    def pick_columns(i, carry):
        at = pl.ds(pl.multiple_of(i * FACE, FACE), FACE)
        out = lax.dot_general(
            s["half"][at, :], s["pick"][...], (((1,), (1,)), ((), ())), preferred_element_type=F32
        )
        s["op2"][at, :] = out.astype(BF16)
        return carry

    came_x()
    came_z = coarse_z(0)
    lax.fori_loop(0, 3, pick_rows, 0)

    came_cut()
    wide_cut = s["all_cut"][...].reshape(ny * 8, s["all_cut"].shape[-1])
    col = lax.broadcasted_iota(jnp.int32, (256, 256), 1)
    row = lax.broadcasted_iota(jnp.int32, (256, 256), 0)
    place = lax.rem(lax.div(col, 8), nx) * group + lax.div(col, 8 * nx) * 6 + lax.rem(col, 8)
    pick = jnp.where((row == place) & (lax.rem(col, 8) < 6), 1.0, 0.0).astype(BF16)
    high, low = split(wide_cut)
    s["inverse"][...] = dot(jnp.concatenate([high, low], axis=0), pick).astype(BF16)

    came_z()
    came_y = coarse_y(0)
    lax.fori_loop(3, 6, pick_rows, 0)
    lax.fori_loop(0, 6, pick_columns, 0)
    came_modes()
    for slot in range(6):
        both = jnp.concatenate([own_modes[slot], s["near_modes"][slot]], axis=0)
        high, low = split(both)
        high, low = high.astype(F32), low.astype(F32)
        tall = jnp.concatenate([high, low, high, jnp.zeros((FACE - 48, FACE), F32)], axis=0)
        s["basis"][slot] = tall.T.astype(BF16)
    came_y()
    came_faces = coarse_faces(0)
    lax.fori_loop(6, 12, pick_columns, 0)
    fetch_disp.wait()
    came_faces()
    lam = s["lam"]
    for slot in range(6):
        lam[slot * FACE : (slot + 1) * FACE, :] = graph(0, slot)

    def operate(k, x, given=None):
        out = fold(dot(s["op2"][...], wide(x)), NB)
        for slot in range(6):
            part = out[slot * FACE : (slot + 1) * FACE, :]
            if given is not None:
                part = (1.0 if slot % 2 else -1.0) * face(given, slot) - part
            s[f"out{k}"][slot] = part
        return to_faces(lambda slot: s[f"out{k}"].at[slot], s[f"in{k}"])

    def assembled(k):
        return (s[f"out{k}"][...] + s[f"in{k}"][...]).reshape(NB, FACE)

    came_halo = operate(1, lam[...], s["disp"])
    scale = s["scale"]
    scale[...] = jnp.ones_like(scale)
    scale[0:1, 0:STORED] = curv[...]
    inverse_curv = 1.0 / scale[0:1, :]
    field_d = s["field_d"]
    for slot in range(6):
        tall = jnp.concatenate([dirs[:, slot, :], jnp.zeros((FACE - STORED, FACE), F32)], axis=0)
        field_d[slot * FACE : (slot + 1) * FACE, :] = tall.T * inverse_curv
    s["dirs3"][...] = thrice(field_d[...])
    for j in range(3):
        high, low = split(images[:, 2 * j + 1, :])
        high, low = high.astype(F32), low.astype(F32)
        s["images2"][j] = jnp.concatenate([high, low], axis=0).astype(BF16)

    came_halo()
    z = s["z"]
    z[...] = assembled(1)
    came_x = coarse_x(1, modes_dot(z[...]))
    came_halo_d = operate(0, field_d[...])
    came_x()
    came_z = coarse_z(1)
    came_z()
    came_y = coarse_y(1)
    came_halo_d()
    zd = s["zd"]
    zd[...] = assembled(0)
    modes_d = modes_dot(zd[...])
    came_y()
    came_faces = coarse_faces(1)
    came_faces()
    w = s["w"]
    for slot in range(6):
        w[slot * FACE : (slot + 1) * FACE, :] = face(z, slot) - graph(1, slot)

    def odd_dot(a, b):
        out = None
        for slot in (1, 3, 5):
            part = jnp.sum(face(a, slot) * face(b, slot), axis=0, keepdims=True)
            out = part if out is None else out + part
        return out

    def stored_dot(a):
        out = None
        for j, slot in enumerate((1, 3, 5)):
            part = dot(s["images2"][j], wide(face(a, slot)))
            out = part if out is None else out + part
        return fold(out, STORED)

    def superstep(k, v, pairs, extra=None):
        came_halo = operate(k, v[...])
        sums = s[f"sums{k}"]
        lines = [odd_dot(a, b) for a, b in pairs]
        lines.append(jnp.zeros((8 - len(lines), FACE), F32))
        flat = jnp.concatenate([stored_dot(v), jnp.concatenate(lines, axis=0), jnp.zeros((16, FACE), F32)], axis=0)
        sums[...] = flat.reshape(8, 8, FACE)
        s[f"sx{k}"][me["gx"]] = sums[me["gx"]]
        came_sx = to_each("gx", sums, s[f"sx{k}"])
        came_halo()
        z[...] = assembled(k)
        c = modes_dot(z[...])
        if extra is not None:
            c = jnp.concatenate([c, extra], axis=1)
        came_x = coarse_x(k, c)
        came_sx()
        s[f"sz{k}"][me["gz"]] = total(s[f"sx{k}"])
        came_sz = to_all("gz", s[f"sz{k}"].at[me["gz"]], s[f"sz{k}"])
        came_x()
        came_z = coarse_z(k)
        came_sz()
        s[f"sy{k}"][me["gy"]] = total(s[f"sz{k}"])
        came_sy = to_all("gy", s[f"sy{k}"].at[me["gy"]], s[f"sy{k}"])
        came_z()
        came_y = coarse_y(k)
        came_sy()
        s[f"all{k}"][me["gx"]] = total(s[f"sy{k}"])
        came_all = to_all("gx", s[f"all{k}"].at[me["gx"]], s[f"all{k}"])
        came_y()
        came_faces = coarse_faces(k)
        came_all()
        return came_faces, s[f"all{k}"][...].reshape(64, FACE)

    def stored_part(gram):
        high, low = split(gram)
        high, low = high.astype(F32), low.astype(F32)
        return jnp.concatenate([high, high, low, jnp.zeros((8, FACE), F32)], axis=0).astype(BF16)

    came_faces, sums = superstep(2, w, (), extra=modes_d)
    gram = sums[0:STORED]
    stack = stored_part(gram)
    p, q, paw = (s["p0"], s["p1"], s["p2"]), (s["q0"], s["q1"], s["q2"]), s["paw"]
    p[0][...] = w[...] - dot(s["dirs3"][...], stack)
    came_faces()
    for slot in range(6):
        at = slice(slot * FACE, (slot + 1) * FACE)
        paw[at, :] = face(z, slot) - graph(2, slot)
        s["pad3"][at, :] = thrice(face(zd, slot) - graph(2, slot, FACE))
    q[0][...] = paw[...] - dot(s["pad3"][...], stack)

    own, curves = [], []
    for k in range(2):
        pairs = [(p[k], q[k]), (p[k], w), (q[k], w), (q[k], q[k])]
        pairs += [(q[j], q[k]) for j in range(k)]
        came_faces, sums = superstep(3 + k, q[k], pairs)
        lines = [sums[STORED + j : STORED + j + 1] for j in range(len(pairs))]
        curves.append(lines[0])
        rate = lines[1] / lines[0]
        own = [own[j] - rate * lines[4 + j] for j in range(k)] + [lines[2] - rate * lines[3]]
        gammas = [own[j] / curves[j] for j in range(k + 1)]
        gram = gram - rate * sums[0:STORED]
        stack = stored_part(gram)
        lam[...] = lam[...] + rate * p[k][...]
        w[...] = w[...] - rate * q[k][...]
        new = w[...] - dot(s["dirs3"][...], stack)
        off = dot(s["pad3"][...], stack)
        for j in range(k + 1):
            new = new - p[j][...] * gammas[j]
            off = off + q[j][...] * gammas[j]
        p[k + 1][...] = new
        q[k + 1][...] = off
        came_faces()
        for slot in range(6):
            at = slice(slot * FACE, (slot + 1) * FACE)
            fresh = paw[at, :] - rate * (face(z, slot) - graph(3 + k, slot))
            paw[at, :] = fresh
            q[k + 1][at, :] = fresh - q[k + 1][at, :]

    lines = jnp.concatenate([odd_dot(p[2], q[2]), odd_dot(p[2], w), jnp.zeros((6, FACE), F32)], axis=0)
    for axis in ("gx", "gz", "gy"):
        buf = s["end_" + axis]
        buf[me[axis]] = lines
        to_all(axis, buf.at[me[axis]], buf)()
        lines = total(buf)
    rate = lines[1:2] / lines[0:1]
    lam_out[...] = lam[...] + rate * p[2][...]
    res_out[...] = w[...] - rate * q[2][...]

    for sem, ref in unsent:
        wait_bytes(ref, sem)


def per_device(sizes, disp, load, flex, bmap, counts, traces, rows, dirs, images, curv):
    nx, ny, nz = sizes
    vmem = pltpu.VMEM
    shapes = {
        "flex": vmem((NB, NB), F32),
        "disp": vmem((NB, FACE), F32),
        "flex2": vmem((NB, 2 * NB), BF16),
        "pick": vmem((NB, NB), BF16),
        "half": vmem((2 * NB, NB), BF16),
        "op2": vmem((2 * NB, NB), BF16),
        "own_rows": vmem((8, 6 * nx * ny * nz), F32),
        "cut": vmem((ny, 8, 256), F32),
        "all_cut": vmem((ny, 8, 256), F32),
        "inverse": vmem((2 * ny * 8, nx * nz * 8), BF16),
        "own_modes": vmem((6, 8, FACE), F32),
        "near_modes": vmem((6, 8, FACE), F32),
        "modes2": vmem((16, NB), BF16),
        "basis": vmem((6, FACE, FACE), BF16),
        "block0": vmem((8, FACE), F32),
        "scale": vmem((8, FACE), F32),
        "dirs3": vmem((NB, FACE), BF16),
        "pad3": vmem((NB, FACE), BF16),
        "images2": vmem((3, 2 * STORED, FACE), BF16),
        "end_gx": vmem((nx, 8, FACE), F32),
        "end_gy": vmem((ny, 8, FACE), F32),
        "end_gz": vmem((nz, 8, FACE), F32),
        "local": pltpu.SemaphoreType.DMA((2,)),
        "sent": pltpu.SemaphoreType.DMA((64,)),
        "came": pltpu.SemaphoreType.DMA((64,)),
    }
    for name in ("lam", "w", "z", "zd", "field_d", "paw", "p0", "p1", "p2", "q0", "q1", "q2"):
        shapes[name] = vmem((NB, FACE), F32)
    for k in range(STEPS):
        width = 2 * FACE if k == 2 else FACE
        shapes[f"out{k}"] = vmem((6, FACE, FACE), F32)
        shapes[f"in{k}"] = vmem((6, FACE, FACE), F32)
        shapes[f"gx{k}"] = vmem((nx, 8, width), F32)
        shapes[f"gz{k}"] = vmem((nz, nx, 8, width), F32)
        shapes[f"part{k}"] = vmem((ny, 8, width), F32)
        shapes[f"gy{k}"] = vmem((ny, 8, width), F32)
        shapes[f"alpha{k}"] = vmem((8, width), F32)
        shapes[f"near{k}"] = vmem((6, 8, width), F32)
        if k >= 2:
            shapes[f"sums{k}"] = vmem((nx, 8, FACE), F32)
            shapes[f"sx{k}"] = vmem((nx, 8, FACE), F32)
            shapes[f"sz{k}"] = vmem((nz, 8, FACE), F32)
            shapes[f"sy{k}"] = vmem((ny, 8, FACE), F32)
            shapes[f"all{k}"] = vmem((nx, 8, FACE), F32)
    names = list(shapes)

    def body(*refs):
        kernel(sizes, *refs[:12], dict(zip(names, refs[12:])))

    inside = pl.BlockSpec(memory_space=pltpu.VMEM)
    outside = pl.BlockSpec(memory_space=pltpu.HBM)
    lam, res = pl.pallas_call(
        body,
        out_shape=[jax.ShapeDtypeStruct((NB, FACE), F32)] * 2,
        in_specs=[
            outside,
            inside,
            outside,
            inside,
            pl.BlockSpec(memory_space=pltpu.SMEM),
            inside,
            inside,
            inside,
            inside,
            inside,
        ],
        out_specs=[inside, inside],
        scratch_shapes=[shapes[n] for n in names],
        compiler_params=pltpu.CompilerParams(
            collective_id=0, has_side_effects=True, vmem_limit_bytes=56 * 1024 * 1024
        ),
        name="feti",
    )(
        disp.reshape(NB, FACE),
        load.reshape(6, FACE),
        flex.reshape(NB, NB),
        bmap.reshape(1, NB),
        counts,
        traces.reshape(6, 6, FACE),
        rows.reshape(6, -1),
        dirs.reshape(STORED, 6, FACE),
        images.reshape(STORED, 6, FACE),
        curv.reshape(1, STORED),
    )
    shape = (1, 1, 1, 6, FACE, FACE)
    return lam.reshape(shape), res.reshape(shape)


def solution(mesh):
    sizes = tuple(mesh.shape[a] for a in AXES)
    cut = P("gx", "gy", "gz")
    return jax.shard_map(
        functools.partial(per_device, sizes),
        mesh=mesh,
        in_specs=(cut,) * 9 + (P(),),
        out_specs=(cut, cut),
        check_vma=False,
    )
```

profile of v0, /device:TPU:1, one launch (start us, length us, event | category | flops | bytes accessed | tf_op | source)
XLA Modules:
  0.0 137.9 jit_solution(6880237492519370032)
XLA Ops:
  1.3 1.3 copy.24
  2.6 1.3 copy.23
  3.9 1.4 %copy.22 = f32[1,1,1,6,1536]{4,3,2,1,0:T(8,128)} copy(f32[1,1,1,6,1536]{4,2,3,1,0:T(1,128)} %param.16) | data formatting | bytes 73728
  5.3 1.7 %copy_bitcast_fusion = (f32[40,6,128]{2,1,0:T(8,128)}, f32[40,6,128]{2,1,0:T(8,128)}) fusion(f32[1,1,1,40,6,128]{5,3,4,2,1,0:T(8,128)} %param.18, f32[1,1,1,40,6,128]{5,3,4,2,1,0:T(8,128)} %param.17), kind=kLoop, calls=%fused_computation | loop fusion | bytes 491520 | tf_op jit(solution)/shard_map/reshape | solution.py:484
  7.0 127.3 %feti.1 = (f32[768,128]{1,0:T(8,128)}, f32[768,128]{1,0:T(8,128)}) custom-call(f32[768,128]{1,0:T(8,128)} %bitcast.20, f32[6,128]{1,0:T(8,128)} %bitcast.25, f32[768,768]{1,0:T(8,128)} %bitcast.19, s32[1,768]{1,0:T(1,128)} %bitcast.26, s32[1,1,1]{2,1,0:T(1,128)S(6)} %copy.27.refs_4_, f32[6,6,128]{2,1,0:T(8,128)} %bitcast.24, f32[6,1536]{1,0:T(8,128)} %bitcast.23, ...), custom_call_target="tpu_custom_call" | custom-call | tf_op jit(solution)/shard_map/feti/pallas_call | solution.py:454
  134.4 1.8 %copy.28 = f32[1,1,1,6,128,128]{5,4,3,2,1,0:T(8,128)} copy(f32[1,1,1,6,128,128]{5,4,3,2,1,0:T(8,128)} %bitcast.22) | data formatting | bytes 786432
  136.1 1.8 %copy.29 = f32[1,1,1,6,128,128]{5,4,3,2,1,0:T(8,128)} copy(f32[1,1,1,6,128,128]{5,4,3,2,1,0:T(8,128)} %bitcast.21) | data formatting | bytes 786432
where the time goes:
time: 138 us
  Pallas kernels  127 us (92%)
  local copies, waits for them, and re-layouts  9.28 us (7%)
    pallas_call x1, Pallas kernels, per_device(): pl.pallas_call(body, out_shape=[jax.ShapeDtypeStruct((NB, FACE), F32)] *...  127 us
    unnamed x5, local copies, waits for them, and re-layouts  7.53 us

commit v1 on v0

v1 whole, which is shorter than its diff:
```python
import functools
from types import SimpleNamespace

import jax
import jax.numpy as jnp
from jax import lax
from jax.experimental import pallas as pl
from jax.experimental.pallas import tpu as pltpu
from jax.sharding import PartitionSpec as P

F32, BF16 = jnp.float32, jnp.bfloat16
GX, GY, GZ = AXES = ("gx", "gy", "gz")
FACE = 128
NB = 6 * FACE
STORED = 40
STEPS = 5
ACROSS = tuple(tuple((1 if slot % 2 else -1) if axis == slot // 2 else 0 for axis in range(3)) for slot in range(6))
ZERO = (0, 0, 0)


def plus(a, b):
    return tuple(i + j for i, j in zip(a, b))


RING = tuple(dict.fromkeys((ZERO, *ACROSS, *(plus(a, b) for a in ACROSS for b in ACROSS))))


def dot(a, b):
    return jnp.dot(a, b, preferred_element_type=F32)


def split(x):
    high = x.astype(BF16)
    return high, (x - high.astype(F32)).astype(BF16)


def wide(x):
    return jnp.concatenate(split(x), axis=1)


def fold(product, rows):
    half = product.shape[1] // 2
    return (product[:rows, :half] + product[:rows, half:]) + product[rows:, :half]


def thrice(x):
    high, low = split(x)
    high, low = high.astype(F32), low.astype(F32)
    return (high + pltpu.roll(low, STORED, 1) + pltpu.roll(high, 2 * STORED, 1)).astype(BF16)


def kernel(sizes, given, lam_out, dir_out, res_out, image_out, rate_out, s):
    nx, ny, nz = sizes
    me = dict(zip(AXES, (lax.axis_index(a) for a in AXES)))
    count = dict(zip(AXES, sizes))
    mesh_id = pl.DeviceIdType.MESH

    def other(axis, delta):
        return lax.rem(me[axis] + (count[axis] + delta), count[axis])

    def at_offset(offset):
        return {axis: other(axis, d) for axis, d in zip(AXES, offset) if d}

    plane = [(dx, 0, dz) for dx in range(nx) for dz in range(nz) if dx or dz]
    line = [(0, dy, 0) for dy in range(1, ny)]
    corner = [o for o in RING if o[1] and (o[0] or o[2])]

    barrier = pltpu.get_barrier_semaphore()
    peers = [at_offset(o) for o in line + plane + corner]
    for peer in peers:
        pl.semaphore_signal(barrier, inc=1, device_id=peer, device_id_type=mesh_id)

    got = s.given
    fetch = {
        name: pltpu.make_async_copy(given[name], got[name], s.local.at[j]) for j, name in enumerate(given)
    }
    for copy in fetch.values():
        copy.start()
    fetch, got = SimpleNamespace(**fetch), SimpleNamespace(**got)

    used = [0]
    unsent = []

    def phase():
        used[0] += 1
        return s.sent.at[used[0] - 1], s.came.at[used[0] - 1]

    def wait_bytes(ref, sem):
        pltpu.make_async_copy(ref, ref, sem).wait()

    def send(src, dst, sems, target):
        pltpu.make_async_remote_copy(
            src_ref=src, dst_ref=dst, send_sem=sems[0], recv_sem=sems[1], device_id=target, device_id_type=mesh_id
        ).start()

    def finish(sems, ref):
        unsent.append((sems[0], ref))
        return lambda: wait_bytes(ref, sems[1])

    def to_faces(piece, dst):
        sems = phase()
        for slot in (2, 3, 4, 5, 0, 1):
            send(piece(slot), dst.at[slot ^ 1], sems, at_offset(ACROSS[slot]))
        return finish(sems, dst)

    def to_all(axis, value, dst):
        sems = phase()
        dst[me[axis]] = value
        for delta in range(1, count[axis]):
            send(dst.at[me[axis]], dst.at[me[axis]], sems, {axis: other(axis, delta)})
        return finish(sems, dst.at[pl.ds(0, count[axis] - 1)])

    def to_each(axis, src, dst):
        sems = phase()
        for delta in range(1, count[axis]):
            peer = other(axis, delta)
            send(src.at[peer], dst.at[me[axis]], sems, {axis: peer})
        dst[me[axis]] = src[me[axis]]
        return finish(sems, dst.at[pl.ds(0, count[axis] - 1)])

    def to_plane(value, dst):
        spot = me[GZ] * nx + me[GX]
        dst[spot] = value
        sems = phase()
        for o in plane:
            send(dst.at[spot], dst.at[spot], sems, at_offset(o))
        return finish(sems, dst.at[pl.ds(0, len(plane))])

    def to_ring(value, dst, reach=len(RING)):
        dst[0] = value
        sems = phase()
        for j in range(1, reach):
            send(dst.at[0], dst.at[j], sems, at_offset(tuple(-d for d in RING[j])))
        return finish(sems, dst.at[pl.ds(1, reach - 1)])

    def total(buf):
        out = buf[0]
        for j in range(1, buf.shape[0]):
            out = out + buf[j]
        return out

    def halves(x):
        high, low = split(x)
        return high.astype(F32), low.astype(F32)

    def slot_rows(slot):
        return slice(slot * FACE, (slot + 1) * FACE)

    def face(ref, slot):
        return ref[slot_rows(slot), :]

    group = nz * 6
    s.own_rows[...] = jnp.zeros_like(s.own_rows)
    s.cut[...] = jnp.zeros_like(s.cut)
    fetch.rows.wait()
    s.own_rows[0:6, :] = got.rows[:, 0, :]
    for j in range(ny):
        for i in range(nx):
            at = (i * ny + j) * group
            s.cut[j, :, i * group : (i + 1) * group] = s.own_rows[:, at : at + group]

    fetch.counts.wait()
    fetch.traces.wait()
    present = lax.broadcasted_iota(jnp.int32, (6, FACE), 0) < got.counts[...]
    own_modes = s.own_modes
    own_modes[...] = jnp.zeros_like(own_modes)
    for slot in range(6):
        sign = 1.0 if slot % 2 else -1.0
        own_modes[slot, 0:6, :] = jnp.where(present, sign * got.traces[:, slot, 0, :], 0.0)

    fetch.load.wait()
    s.block0[...] = jnp.zeros_like(s.block0)
    s.block0[0:6, :] = got.load[:, 0, :]

    pl.semaphore_wait(barrier, len(peers))

    def by_lanes(width, f):
        parts = [f(slice(at, at + FACE)) for at in range(0, width, FACE)]
        return parts[0] if len(parts) == 1 else jnp.concatenate(parts, axis=1)

    def coarse_y(k):
        width = s.plane[k].shape[-1]
        c = s.plane[k][...].reshape(nx * nz * 8, width)
        partial = by_lanes(width, lambda at: fold(dot(s.inverse[...], wide(c[:, at])), ny * 8))
        s.part[k][...] = partial.reshape(ny, 8, width)
        return to_each(GY, s.part[k], s.gy[k])

    def graph(k, slot, at=slice(0, FACE)):
        own = s.ring[k][0, :, at]
        near = s.ring[k][1 + slot, :, at]
        high, low = halves(jnp.concatenate([own, near], axis=0))
        stack = jnp.concatenate([high, high, low, jnp.zeros((FACE - 48, FACE), F32)], axis=0).astype(BF16)
        return dot(s.basis[slot], stack)

    def modes_dot(z):
        return fold(dot(s.modes2[...], wide(z)), 8)

    def apply(x):
        return fold(dot(s.op2[...], wide(x)), NB)

    def spread(r, k):
        own = None
        for slot in range(6):
            part = fold(dot(s.both2[slot], wide(r[slot_rows(slot), :])), 16)
            own = part[0:8] if own is None else own + part[0:8]
            s.share[k][slot] = part[8:16]
        came = to_faces(lambda slot: s.share[k].at[slot], s.shares[k])
        s.mine[k][...] = own
        return came

    def gathered(k):
        return s.mine[k][...] + total(s.shares[k])

    def stencil(k):
        width = s.ring[k].shape[-1]
        a = s.ring[k][...].reshape(256, width)
        return by_lanes(width, lambda at: fold(dot(s.stencil2[...], wide(a[:, at])), 8))

    def operate(k, x, load=None):
        out = apply(x)
        for slot in range(6):
            part = out[slot_rows(slot), :]
            if load is not None:
                part = (1.0 if slot % 2 else -1.0) * face(load, slot) - part
            s.out[k][slot] = part
        return to_faces(lambda slot: s.out[k].at[slot], s.halo[k])

    def assembled(k):
        return (s.out[k][...] + s.halo[k][...]).reshape(NB, FACE)

    came_cut = to_each(GY, s.cut, s.all_cut)
    came_plane = to_plane(s.block0[...], s.plane[0])
    came_modes = to_faces(lambda slot: own_modes.at[slot], s.near_modes)

    modes = jnp.concatenate([own_modes[slot] for slot in range(6)], axis=1)
    s.modes2[...] = jnp.concatenate(halves(modes), axis=0).astype(BF16)
    for k in range(STEPS - 1):
        tail = s.ring[k].shape
        s.ring[k][len(RING) :] = jnp.zeros((tail[0] - len(RING), *tail[1:]), F32)

    fetch.flex.wait()
    fetch.bmap.wait()

    def cut_flex(i, carry):
        at = pl.ds(pl.multiple_of(i * FACE, FACE), FACE)
        high, low = split(got.flex[at, :])
        s.flex2[at, 0:NB] = high
        s.flex2[at, NB : 2 * NB] = low
        sign = lax.convert_element_type(2 * lax.rem(i, 2) - 1, F32)
        spot = i * FACE + lax.broadcasted_iota(jnp.int32, (FACE, NB), 0)
        s.pick[at, :] = jnp.where(got.bmap[...] == spot, sign, 0.0).astype(BF16)
        return carry

    def pick_rows(i, carry):
        at = pl.multiple_of(i * FACE, FACE)
        out = dot(s.pick[pl.ds(at, FACE), :], s.flex2[...])
        s.half[pl.ds(at, FACE), :] = out[:, 0:NB].astype(BF16)
        s.half[pl.ds(NB + at, FACE), :] = out[:, NB : 2 * NB].astype(BF16)
        return carry

    def pick_columns(i, carry):
        at = pl.ds(pl.multiple_of(i * 2 * FACE, 2 * FACE), 2 * FACE)
        out = lax.dot_general(s.half[at, :], s.pick[...], (((1,), (1,)), ((), ())), preferred_element_type=F32)
        s.op2[at, :] = out.astype(BF16)
        return carry

    lax.fori_loop(0, 6, cut_flex, 0)
    lax.fori_loop(0, 6, pick_rows, 0)

    came_cut()
    wide_cut = s.all_cut[...].reshape(ny * 8, s.all_cut.shape[-1])
    col = lax.broadcasted_iota(jnp.int32, (256, 256), 1)
    row = lax.broadcasted_iota(jnp.int32, (256, 256), 0)
    place = lax.rem(lax.div(col, 8), nx) * group + lax.div(col, 8 * nx) * 6 + lax.rem(col, 8)
    pick = jnp.where((row == place) & (lax.rem(col, 8) < 6), 1.0, 0.0).astype(BF16)
    s.inverse[...] = dot(jnp.concatenate(split(wide_cut), axis=0), pick).astype(BF16)

    lax.fori_loop(0, 6, pick_columns, 0)
    came_plane()
    came_y = coarse_y(0)

    came_modes()
    for slot in range(6):
        own, near = own_modes[slot], s.near_modes[slot]
        high, low = halves(jnp.concatenate([own, near], axis=0))
        s.both2[slot] = jnp.concatenate([high, low], axis=0).astype(BF16)
        tall = jnp.concatenate([high, low, high, jnp.zeros((FACE - 48, FACE), F32)], axis=0)
        s.basis[slot] = tall.T.astype(BF16)
        blank = [own] + [jnp.zeros((8, FACE), F32)] * 15
        blank[1 + slot] = near
        s.field_g[slot_rows(slot), :] = jnp.concatenate(blank, axis=0).T
    came_share = spread(apply(s.field_g[...]), 0)
    fetch.disp.wait()
    signed = [(1.0 if slot % 2 else -1.0) * face(got.disp, slot) for slot in range(6)]
    came_load = spread(jnp.concatenate(signed, axis=0), 1)
    came_y()
    came_ring = to_ring(total(s.gy[0]), s.ring[0])

    came_share()
    lane = lax.broadcasted_iota(jnp.int32, (8, FACE), 1)
    parts = [jnp.zeros((8, FACE), F32)] * 2
    for j, base in enumerate((ZERO, *ACROSS)):
        source = s.mine[0][...] if j == 0 else s.shares[0][j - 1]
        for b, step in enumerate((ZERO, *ACROSS)):
            to = RING.index(plus(base, step))
            moved = pltpu.roll(source, (8 * (to % 16) - 8 * b) % FACE, 1)
            parts[to // 16] = parts[to // 16] + jnp.where(lax.div(lane, 8) == to % 16, moved, 0.0)
    s.stencil2[...] = jnp.concatenate(halves(jnp.concatenate(parts, axis=1)), axis=0).astype(BF16)
    came_load()
    came_ring()
    came_plane = to_plane(gathered(1) - stencil(0), s.plane[1])

    lam, w, z, zd, paw = s.lam, s.w, s.z, s.zd, s.paw
    for slot in range(6):
        lam[slot_rows(slot), :] = graph(0, slot)
    came_halo = operate(1, lam[...], got.disp)
    fetch.dirs.wait()
    fetch.curv.wait()
    fetch.images.wait()
    s.scale[...] = jnp.ones_like(s.scale)
    s.scale[0:1, 0:STORED] = got.curv[...]
    inverse_curv = 1.0 / s.scale[0:1, :]
    for slot in range(6):
        tall = jnp.concatenate([got.dirs[slot], jnp.zeros((FACE - STORED, FACE), F32)], axis=0)
        s.field_d[slot_rows(slot), :] = tall.T * inverse_curv
    came_halo_d = operate(0, s.field_d[...])
    came_plane()
    came_y = coarse_y(1)
    came_halo()
    z[...] = assembled(1)
    came_share = spread(apply(z[...]), 2)
    s.dirs3[...] = thrice(s.field_d[...])
    for j in range(3):
        s.images2[j] = jnp.concatenate(halves(got.images[2 * j + 1]), axis=0).astype(BF16)
    came_y()
    came_ring = to_ring(total(s.gy[1]), s.ring[1])
    came_halo_d()
    zd[...] = assembled(0)
    modes_d = modes_dot(zd[...])
    came_share()
    start = gathered(2)
    came_ring()
    came_plane = to_plane(jnp.concatenate([start - stencil(1), modes_d], axis=1), s.plane[2])
    for slot in range(6):
        w[slot_rows(slot), :] = face(z, slot) - graph(1, slot)

    def odd_dot(a, b):
        out = None
        for slot in (1, 3, 5):
            part = jnp.sum(face(a, slot) * face(b, slot), axis=0, keepdims=True)
            out = part if out is None else out + part
        return out

    def stored_dot(a):
        out = None
        for j, slot in enumerate((1, 3, 5)):
            part = dot(s.images2[j], wide(face(a, slot)))
            out = part if out is None else out + part
        return fold(out, STORED)

    def superstep(k, v, pairs, came_plane):
        j = k - 2
        lines = [odd_dot(a, b) for a, b in pairs]
        lines.append(jnp.zeros((8 - len(lines), FACE), F32))
        flat = jnp.concatenate([stored_dot(v), *lines, jnp.zeros((16, FACE), F32)], axis=0)
        s.sums[j][...] = flat.reshape(8, 8, FACE)
        came_sums = to_each(GY, s.sums[j], s.sums_y[j])
        came_halo = operate(k, v[...])
        came_plane()
        came_y = coarse_y(k)
        came_sums()
        came_sums = to_plane(total(s.sums_y[j]), s.sums_plane[j])
        came_d = spread(apply(zd[...]), 3) if k == 2 else None
        came_halo()
        z[...] = assembled(k)
        came_share = spread(apply(z[...]), k + 2) if k < 4 else None
        came_y()
        came_ring = to_ring(total(s.gy[k]), s.ring[k], len(RING) if k < 4 else 7)
        came_sums()
        came_sums = to_all(GY, total(s.sums_plane[j]), s.sums_all[j])
        for came in (came_d, came_share):
            if came is not None:
                came()
        return came_ring, came_sums, s.sums_all[j]

    def stored_part(gram):
        high, low = halves(gram)
        return jnp.concatenate([high, high, low, jnp.zeros((8, FACE), F32)], axis=0).astype(BF16)

    p, q = s.p, s.q
    came_ring, came_sums, sums = superstep(2, w, (), came_plane)
    came_ring()
    off = stencil(2)
    modes_paw = gathered(4) - off[:, 0:FACE]
    modes_pad3 = thrice(gathered(3) - off[:, FACE:])
    for slot in range(6):
        at = slot_rows(slot)
        paw[at, :] = face(z, slot) - graph(2, slot)
        s.pad3[at, :] = thrice(face(zd, slot) - graph(2, slot, slice(FACE, 2 * FACE)))
    came_sums()
    gram = sums[...].reshape(64, FACE)[0:STORED]
    stack = stored_part(gram)
    modes_q = [modes_paw - dot(modes_pad3, stack)]
    came_plane = to_plane(modes_q[0], s.plane[3])
    q[0][...] = paw[...] - dot(s.pad3[...], stack)
    p[0][...] = w[...] - dot(s.dirs3[...], stack)

    own, curves = [], []
    for k in range(2):
        pairs = [(p[k], q[k]), (p[k], w), (q[k], w), (q[k], q[k])]
        pairs += [(q[j], q[k]) for j in range(k)]
        came_ring, came_sums, sums = superstep(3 + k, q[k], pairs, came_plane)
        if k == 0:
            came_ring()
            change = gathered(5) - stencil(3)
        came_sums()
        sums = sums[...].reshape(64, FACE)
        lines = [sums[STORED + j : STORED + j + 1] for j in range(len(pairs))]
        curves.append(lines[0])
        rate = lines[1] / lines[0]
        own = [own[j] - rate * lines[4 + j] for j in range(k)] + [lines[2] - rate * lines[3]]
        gammas = [own[j] / curves[j] for j in range(k + 1)]
        gram = gram - rate * sums[0:STORED]
        stack = stored_part(gram)
        if k == 0:
            modes_paw = modes_paw - rate * change
            came_plane = to_plane(modes_paw - dot(modes_pad3, stack) - gammas[0] * modes_q[0], s.plane[4])
            for slot in range(6):
                at = slot_rows(slot)
                paw[at, :] = paw[at, :] - rate * (face(z, slot) - graph(3, slot))
        lam[...] = lam[...] + rate * p[k][...]
        w[...] = w[...] - rate * q[k][...]
        new = w[...] - dot(s.dirs3[...], stack)
        off = dot(s.pad3[...], stack)
        for j in range(k + 1):
            new = new - p[j][...] * gammas[j]
            off = off + q[j][...] * gammas[j]
        p[k + 1][...] = new
        if k == 0:
            q[1][...] = paw[...] - off

    over = rate * jnp.sum(modes_dot(p[2][...]) * s.ring[4][0], axis=0, keepdims=True)
    q[2][...] = paw[...] - off
    for slot in (1, 3, 5):
        known = face(q[2], slot) - rate * face(z, slot)
        over = over + jnp.sum(face(p[2], slot) * known, axis=0, keepdims=True)
    lines = jnp.concatenate([over, odd_dot(p[2], w), jnp.zeros((6, FACE), F32)], axis=0)
    came_end = to_plane(lines, s.end_plane)
    came_ring()
    for slot in range(6):
        at = slot_rows(slot)
        image_out[at, :] = q[2][at, :] - rate * (face(z, slot) - graph(4, slot))

    lam_out[...] = lam[...]
    dir_out[...] = p[2][...]
    res_out[...] = w[...]
    came_end()
    to_all(GY, total(s.end_plane), s.end_gy)()
    lines = total(s.end_gy)
    rate_out[...] = lines[1:2] / lines[0:1]

    for sem, ref in unsent:
        wait_bytes(ref, sem)


def per_device(sizes, disp, load, flex, bmap, counts, traces, rows, dirs, images, curv):
    nx, ny, nz = sizes
    vmem = pltpu.VMEM
    given = dict(
        rows=rows.reshape(6, 1, -1),
        load=load.reshape(6, 1, FACE),
        counts=counts.reshape(1, 1),
        traces=traces.reshape(6, 6, 1, FACE),
        flex=flex.reshape(NB, NB),
        bmap=bmap.reshape(1, NB),
        disp=disp.reshape(NB, FACE),
        dirs=dirs.reshape(STORED, 6, FACE).swapaxes(0, 1),
        curv=curv.reshape(1, STORED),
        images=images.reshape(STORED, 6, FACE).swapaxes(0, 1),
    )
    widths = [2 * FACE if k == 2 else FACE for k in range(STEPS)]
    field = vmem((NB, FACE), F32)
    blocks = lambda n, width=FACE: vmem((n, 8, width), F32)
    scratch = dict(
        given={name: vmem(x.shape, x.dtype) for name, x in given.items()},
        flex2=vmem((NB, 2 * NB), BF16),
        pick=vmem((NB, NB), BF16),
        half=vmem((2 * NB, NB), BF16),
        op2=vmem((2 * NB, NB), BF16),
        own_rows=vmem((8, 6 * nx * ny * nz), F32),
        cut=blocks(ny, 256),
        all_cut=blocks(ny, 256),
        inverse=vmem((2 * ny * 8, nx * nz * 8), BF16),
        own_modes=blocks(6),
        near_modes=blocks(6),
        modes2=vmem((16, NB), BF16),
        both2=vmem((6, 32, FACE), BF16),
        stencil2=vmem((16, 256), BF16),
        basis=vmem((6, FACE, FACE), BF16),
        block0=vmem((8, FACE), F32),
        scale=vmem((8, FACE), F32),
        dirs3=vmem((NB, FACE), BF16),
        pad3=vmem((NB, FACE), BF16),
        images2=vmem((3, 2 * STORED, FACE), BF16),
        end_plane=blocks(nx * nz),
        end_gy=blocks(ny),
        lam=field,
        w=field,
        z=field,
        zd=field,
        field_d=field,
        field_g=field,
        paw=field,
        p=[field] * 3,
        q=[field] * 3,
        out=[vmem((6, FACE, FACE), F32)] * STEPS,
        halo=[vmem((6, FACE, FACE), F32)] * STEPS,
        plane=[blocks(nx * nz, width) for width in widths],
        part=[blocks(ny, width) for width in widths],
        gy=[blocks(ny, width) for width in widths],
        ring=[blocks(32, width) for width in widths],
        share=[blocks(6)] * 6,
        shares=[blocks(6)] * 6,
        mine=[vmem((8, FACE), F32)] * 6,
        sums=[blocks(ny)] * 3,
        sums_y=[blocks(ny)] * 3,
        sums_plane=[blocks(nx * nz)] * 3,
        sums_all=[blocks(ny)] * 3,
        local=pltpu.SemaphoreType.DMA((len(given),)),
        sent=pltpu.SemaphoreType.DMA((64,)),
        came=pltpu.SemaphoreType.DMA((64,)),
    )
    leaves, tree = jax.tree.flatten(scratch, is_leaf=lambda x: not isinstance(x, (dict, list)))

    def body(*refs):
        cut = len(given)
        held = SimpleNamespace(**jax.tree.unflatten(tree, refs[cut + 5 :]))
        kernel(sizes, dict(zip(given, refs[:cut])), *refs[cut : cut + 5], held)

    inside = pl.BlockSpec(memory_space=pltpu.VMEM)
    outside = pl.BlockSpec(memory_space=pltpu.HBM)
    lam, direction, res, image, rate = pl.pallas_call(
        body,
        out_shape=[jax.ShapeDtypeStruct((NB, FACE), F32)] * 4 + [jax.ShapeDtypeStruct((1, FACE), F32)],
        in_specs=[outside] * len(given),
        out_specs=[inside] * 5,
        scratch_shapes=leaves,
        compiler_params=pltpu.CompilerParams(
            collective_id=0, has_side_effects=True, vmem_limit_bytes=56 * 1024 * 1024
        ),
        name="feti",
    )(*given.values())
    shape = (1, 1, 1, 6, FACE, FACE)
    return (lam + rate * direction).reshape(shape), (res - rate * image).reshape(shape)


def solution(mesh):
    sizes = tuple(mesh.shape[a] for a in AXES)
    cut = P("gx", "gy", "gz")
    return jax.shard_map(
        functools.partial(per_device, sizes),
        mesh=mesh,
        in_specs=(cut,) * 9 + (P(),),
        out_specs=(cut, cut),
        check_vma=False,
    )
```

time: 138 us -> 107 us (0.78)
  Pallas kernels: 127 us -> 103 us
  local copies, waits for them, and re-layouts: 9.28 us -> 0 us
  other arithmetic: 0 us -> 2.31 us
    pallas_call x1, Pallas kernels: 127 us -> 103 us  [per_device(): pl.pallas_call(body, out_shape=[jax.ShapeDtypeStruct((NB, FACE), F32)] *...]
    unnamed x5 -> x0, local copies, waits for them, and re-layouts: 7.53 us -> none
    sub x0 -> x1, other arithmetic: none -> 2.31 us  [per_device(): res - rate * image]
    reshape x1 -> x0, local copies, waits for them, and re-layouts: 1.74 us -> none  [per_device(): images.reshape(STORED, 6, FACE)]
where the time goes in v1:
time: 107 us
  Pallas kernels  103 us (96%)
  other arithmetic  2.31 us (2%)
  between operations  1.29 us (1%)
    pallas_call x1, Pallas kernels, per_device(): pl.pallas_call(body, out_shape=[jax.ShapeDtypeStruct((NB, FACE), F32)] *...  103 us
    sub x1, other arithmetic, per_device(): res - rate * image  2.31 us

profile of v1, /device:TPU:1, one launch (start us, length us, event | category | flops | bytes accessed | tf_op | source)
XLA Modules:
  0.0 106.7 jit_solution(4262464622512003697)
XLA Ops:
  1.3 103.1 %feti.1 = (f32[768,128]{1,0:T(8,128)}, f32[768,128]{1,0:T(8,128)}, f32[768,128]{1,0:T(8,128)}, f32[768,128]{1,0:T(8,128)}, f32[1,128]{1,0:T(1,128)}) custom-call(f32[6,1,1536]{2,1,0:T(1,128)} %bitcast.24, f32[6,1,128]{2,1,0:T(1,128)} %bitcast.26, s32[1,1]{1,0:T(1,128)} %bitcast.17.refs_2_, f32[6,6,1,128]{3,2,1,0:T(1,128)} %bitcast.25, f32[768,768]{1,0:T(8,128)} %bitcast.18, ...), custom_call_target="tpu_custom_call" | custom-call | tf_op jit(solution)/shard_map/feti/pallas_call | solution.py:542
  104.4 2.3 %multiply_subtract_fusion = (f32[768,128]{1,0:T(8,128)}, f32[768,128]{1,0:T(8,128)}) fusion(f32[768,128]{1,0:T(8,128)} %get-tuple-element.10, f32[768,128]{1,0:T(8,128)} %get-tuple-element.11, f32[128]{0:T(128)} %bitcast.28, f32[768,128]{1,0:T(8,128)} %get-tuple-element.7, f32[768,128]{1,0:T(8,128)} %get-tuple-element.9), kind=kLoop, calls=%fused_computation | loop fusion | flops 393216 | bytes 2359808 | tf_op jit(solution)/shard_map/sub | solution.py:554

commit v2 on v1

--- a/solution.py
+++ b/solution.py
@@ -13,7 +13,8 @@
 FACE = 128
 NB = 6 * FACE
 STORED = 40
-STEPS = 5
+STEPS = 6
+STORED_STEP = 5
 ACROSS = tuple(tuple((1 if slot % 2 else -1) if axis == slot // 2 else 0 for axis in range(3)) for slot in range(6))
 ZERO = (0, 0, 0)
 
@@ -174,20 +175,14 @@
 
     pl.semaphore_wait(barrier, len(peers))
 
-    def by_lanes(width, f):
-        parts = [f(slice(at, at + FACE)) for at in range(0, width, FACE)]
-        return parts[0] if len(parts) == 1 else jnp.concatenate(parts, axis=1)
-
     def coarse_y(k):
-        width = s.plane[k].shape[-1]
-        c = s.plane[k][...].reshape(nx * nz * 8, width)
-        partial = by_lanes(width, lambda at: fold(dot(s.inverse[...], wide(c[:, at])), ny * 8))
-        s.part[k][...] = partial.reshape(ny, 8, width)
+        c = s.plane[k][...].reshape(nx * nz * 8, FACE)
+        s.part[k][...] = fold(dot(s.inverse[...], wide(c)), ny * 8).reshape(ny, 8, FACE)
         return to_each(GY, s.part[k], s.gy[k])
 
-    def graph(k, slot, at=slice(0, FACE)):
-        own = s.ring[k][0, :, at]
-        near = s.ring[k][1 + slot, :, at]
+    def graph(k, slot):
+        own = s.ring[k][0]
+        near = s.ring[k][1 + slot]
         high, low = halves(jnp.concatenate([own, near], axis=0))
         stack = jnp.concatenate([high, high, low, jnp.zeros((FACE - 48, FACE), F32)], axis=0).astype(BF16)
         return dot(s.basis[slot], stack)
@@ -212,9 +207,7 @@
         return s.mine[k][...] + total(s.shares[k])
 
     def stencil(k):
-        width = s.ring[k].shape[-1]
-        a = s.ring[k][...].reshape(256, width)
-        return by_lanes(width, lambda at: fold(dot(s.stencil2[...], wide(a[:, at])), 8))
+        return fold(dot(s.stencil2[...], wide(s.ring[k][...].reshape(256, FACE))), 8)
 
     def operate(k, x, load=None):
         out = apply(x)
@@ -234,7 +227,7 @@
 
     modes = jnp.concatenate([own_modes[slot] for slot in range(6)], axis=1)
     s.modes2[...] = jnp.concatenate(halves(modes), axis=0).astype(BF16)
-    for k in range(STEPS - 1):
+    for k in (0, 1, 2, 3, STORED_STEP):
         tail = s.ring[k].shape
         s.ring[k][len(RING) :] = jnp.zeros((tail[0] - len(RING), *tail[1:]), F32)
 
@@ -266,6 +259,7 @@
 
     lax.fori_loop(0, 6, cut_flex, 0)
     lax.fori_loop(0, 6, pick_rows, 0)
+    lax.fori_loop(0, 6, pick_columns, 0)
 
     came_cut()
     wide_cut = s.all_cut[...].reshape(ny * 8, s.all_cut.shape[-1])
@@ -275,7 +269,6 @@
     pick = jnp.where((row == place) & (lax.rem(col, 8) < 6), 1.0, 0.0).astype(BF16)
     s.inverse[...] = dot(jnp.concatenate(split(wide_cut), axis=0), pick).astype(BF16)
 
-    lax.fori_loop(0, 6, pick_columns, 0)
     came_plane()
     came_y = coarse_y(0)
 
@@ -329,18 +322,58 @@
     came_halo()
     z[...] = assembled(1)
     came_share = spread(apply(z[...]), 2)
-    s.dirs3[...] = thrice(s.field_d[...])
-    for j in range(3):
-        s.images2[j] = jnp.concatenate(halves(got.images[2 * j + 1]), axis=0).astype(BF16)
-    came_y()
-    came_ring = to_ring(total(s.gy[1]), s.ring[1])
     came_halo_d()
     zd[...] = assembled(0)
-    modes_d = modes_dot(zd[...])
+    came_plane_d = to_plane(modes_dot(zd[...]), s.plane[STORED_STEP])
+    s.dirs3[...] = thrice(s.field_d[...])
+    modes_of_images = None
+    for slot in range(6):
+        tall = jnp.concatenate([own_modes[slot], jnp.zeros((FACE - 8, FACE), F32)], axis=0)
+        part = lax.dot_general(
+            got.images[slot],
+            tall,
+            (((1,), (1,)), ((), ())),
+            precision=lax.Precision.HIGHEST,
+            preferred_element_type=F32,
+        )
+        modes_of_images = part if slot == 0 else modes_of_images + part
+        if slot % 2:
+            s.images2[slot // 2] = jnp.concatenate(halves(got.images[slot]), axis=0).astype(BF16)
+    s.images2[3] = jnp.concatenate(halves(modes_of_images), axis=0).astype(BF16)
+
+    class StoredSums:
+        def __init__(self, j, field, alpha):
+            self.j = j
+            parts = [field[slot_rows(slot), :] for slot in (1, 3, 5)]
+            parts.append(jnp.concatenate([-alpha, jnp.zeros((FACE - 8, FACE), F32)], axis=0))
+            out = None
+            for i, part in enumerate(parts):
+                term = dot(s.images2[i], wide(part))
+                out = term if out is None else out + term
+            flat = jnp.concatenate([fold(out, STORED), jnp.zeros((64 - STORED, FACE), F32)], axis=0)
+            s.sums[j][...] = flat.reshape(8, 8, FACE)
+            self.came = to_each(GY, s.sums[j], s.sums_y[j])
+
+        def share(self):
+            self.came()
+            self.came = to_plane(total(s.sums_y[self.j]), s.sums_plane[self.j])
+
+        def collect(self):
+            self.came()
+            self.came = to_all(GY, total(s.sums_plane[self.j]), s.sums_all[self.j])
+
+        def result(self):
+            self.came()
+            return s.sums_all[self.j][...].reshape(64, FACE)[0:STORED]
+
+    came_y()
+    alpha = total(s.gy[1])
+    came_ring = to_ring(alpha, s.ring[1])
+    sums_w = StoredSums(0, z[...], alpha)
     came_share()
     start = gathered(2)
     came_ring()
-    came_plane = to_plane(jnp.concatenate([start - stencil(1), modes_d], axis=1), s.plane[2])
+    came_plane = to_plane(start - stencil(1), s.plane[2])
     for slot in range(6):
         w[slot_rows(slot), :] = face(z, slot) - graph(1, slot)
 
@@ -351,57 +384,68 @@
             out = part if out is None else out + part
         return out
 
-    def stored_dot(a):
-        out = None
-        for j, slot in enumerate((1, 3, 5)):
-            part = dot(s.images2[j], wide(face(a, slot)))
-            out = part if out is None else out + part
-        return fold(out, STORED)
-
-    def superstep(k, v, pairs, came_plane):
-        j = k - 2
-        lines = [odd_dot(a, b) for a, b in pairs]
-        lines.append(jnp.zeros((8 - len(lines), FACE), F32))
-        flat = jnp.concatenate([stored_dot(v), *lines, jnp.zeros((16, FACE), F32)], axis=0)
-        s.sums[j][...] = flat.reshape(8, 8, FACE)
-        came_sums = to_each(GY, s.sums[j], s.sums_y[j])
+    def superstep(k, v, pairs, came_plane, sums):
+        j = k - 3
+        came_pairs, came_d, came_share, sums_d, sums_z = None, None, None, None, None
+        if pairs:
+            lines = [odd_dot(a, b) for a, b in pairs]
+            lines.append(jnp.zeros((8 - len(lines), FACE), F32))
+            came_pairs = to_all(GY, jnp.concatenate(lines, axis=0), s.pairs_y[j])
+        sums[0].share()
         came_halo = operate(k, v[...])
+        if k == 2:
+            came_plane_d()
+            came_y_d = coarse_y(STORED_STEP)
         came_plane()
         came_y = coarse_y(k)
-        came_sums()
-        came_sums = to_plane(total(s.sums_y[j]), s.sums_plane[j])
-        came_d = spread(apply(zd[...]), 3) if k == 2 else None
+        if pairs:
+            came_pairs()
+            came_pairs = to_plane(total(s.pairs_y[j]), s.pairs_plane[j])
+        for each in sums:
+            each.collect()
+        if k == 2:
+            came_d = spread(apply(zd[...]), 3)
         came_halo()
         z[...] = assembled(k)
-        came_share = spread(apply(z[...]), k + 2) if k < 4 else None
+        if k == 2:
+            came_y_d()
+            alpha = total(s.gy[STORED_STEP])
+            came_ring_d = to_ring(alpha, s.ring[STORED_STEP])
+            sums_d = StoredSums(1, zd[...], alpha)
+        if k < 4:
+            came_share = spread(apply(z[...]), k + 2)
         came_y()
-        came_ring = to_ring(total(s.gy[k]), s.ring[k], len(RING) if k < 4 else 7)
-        came_sums()
-        came_sums = to_all(GY, total(s.sums_plane[j]), s.sums_all[j])
-        for came in (came_d, came_share):
-            if came is not None:
-                came()
-        return came_ring, came_sums, s.sums_all[j]
+        alpha = total(s.gy[k])
+        came_ring = to_ring(alpha, s.ring[k], len(RING) if k < 4 else 7)
+        if k < 4:
+            sums_z = StoredSums(k, z[...], alpha)
+        if k == 2:
+            sums_d.share()
+            came_d()
+            came_ring_d()
+        if k < 4:
+            came_share()
+        return came_ring, came_pairs, [x for x in (sums_z, sums_d) if x is not None]
 
     def stored_part(gram):
         high, low = halves(gram)
         return jnp.concatenate([high, high, low, jnp.zeros((8, FACE), F32)], axis=0).astype(BF16)
 
     p, q = s.p, s.q
-    came_ring, came_sums, sums = superstep(2, w, (), came_plane)
+    came_ring, _, later = superstep(2, w, (), came_plane, [sums_w])
+    modes_pad3 = thrice(gathered(3) - stencil(STORED_STEP))
+    gram = sums_w.result()
+    stack = stored_part(gram)
+    modes_off = gathered(4) - dot(modes_pad3, stack)
     came_ring()
-    off = stencil(2)
-    modes_paw = gathered(4) - off[:, 0:FACE]
-    modes_pad3 = thrice(gathered(3) - off[:, FACE:])
+    change = stencil(2)
+    modes_q = modes_off - change
+    modes_paw = gathered(4) - change
+    came_plane = to_plane(modes_q, s.plane[3])
     for slot in range(6):
         at = slot_rows(slot)
         paw[at, :] = face(z, slot) - graph(2, slot)
-        s.pad3[at, :] = thrice(face(zd, slot) - graph(2, slot, slice(FACE, 2 * FACE)))
-    came_sums()
-    gram = sums[...].reshape(64, FACE)[0:STORED]
-    stack = stored_part(gram)
-    modes_q = [modes_paw - dot(modes_pad3, stack)]
-    came_plane = to_plane(modes_q[0], s.plane[3])
+        s.pad3[at, :] = thrice(face(zd, slot) - graph(STORED_STEP, slot))
     q[0][...] = paw[...] - dot(s.pad3[...], stack)
     p[0][...] = w[...] - dot(s.dirs3[...], stack)
 
@@ -409,26 +453,26 @@
     for k in range(2):
         pairs = [(p[k], q[k]), (p[k], w), (q[k], w), (q[k], q[k])]
         pairs += [(q[j], q[k]) for j in range(k)]
-        came_ring, came_sums, sums = superstep(3 + k, q[k], pairs, came_plane)
+        came_ring, came_pairs, latest = superstep(3 + k, q[k], pairs, came_plane, later)
+        came_pairs()
+        sums = total(s.pairs_plane[k])
+        lines = [sums[j : j + 1] for j in range(len(pairs))]
         if k == 0:
-            came_ring()
-            change = gathered(5) - stencil(3)
-        came_sums()
-        sums = sums[...].reshape(64, FACE)
-        lines = [sums[STORED + j : STORED + j + 1] for j in range(len(pairs))]
+            gram_paw = later[0].result()
+            gram_pad3 = thrice(later[1].result())
+            gram_q = gram_paw - dot(gram_pad3, stack)
+        else:
+            gram_paw = gram_paw - rate * later[0].result()
+            gram_q = gram_paw - dot(gram_pad3, stack) - gammas[0] * gram_q
+        later = latest
         curves.append(lines[0])
         rate = lines[1] / lines[0]
         own = [own[j] - rate * lines[4 + j] for j in range(k)] + [lines[2] - rate * lines[3]]
         gammas = [own[j] / curves[j] for j in range(k + 1)]
-        gram = gram - rate * sums[0:STORED]
+        gram = gram - rate * gram_q
         stack = stored_part(gram)
         if k == 0:
-            modes_paw = modes_paw - rate * change
-            came_plane = to_plane(modes_paw - dot(modes_pad3, stack) - gammas[0] * modes_q[0], s.plane[4])
-            for slot in range(6):
-                at = slot_rows(slot)
-                paw[at, :] = paw[at, :] - rate * (face(z, slot) - graph(3, slot))
-        lam[...] = lam[...] + rate * p[k][...]
+            modes_off = modes_paw - rate * gathered(5) - dot(modes_pad3, stack) - gammas[0] * modes_q
         w[...] = w[...] - rate * q[k][...]
         new = w[...] - dot(s.dirs3[...], stack)
         off = dot(s.pad3[...], stack)
@@ -436,8 +480,16 @@
             new = new - p[j][...] * gammas[j]
             off = off + q[j][...] * gammas[j]
         p[k + 1][...] = new
+        lam[...] = lam[...] + rate * p[k][...]
         if k == 0:
-            q[1][...] = paw[...] - off
+            q[1][...] = paw[...] - rate * z[...] - off
+            came_ring()
+            came_plane = to_plane(modes_off + rate * stencil(3), s.plane[4])
+            for slot in range(6):
+                at = slot_rows(slot)
+                change = rate * graph(3, slot)
+                paw[at, :] = paw[at, :] - rate * face(z, slot) + change
+                q[1][at, :] = q[1][at, :] + change
 
     over = rate * jnp.sum(modes_dot(p[2][...]) * s.ring[4][0], axis=0, keepdims=True)
     q[2][...] = paw[...] - off
@@ -478,7 +530,6 @@
         curv=curv.reshape(1, STORED),
         images=images.reshape(STORED, 6, FACE).swapaxes(0, 1),
     )
-    widths = [2 * FACE if k == 2 else FACE for k in range(STEPS)]
     field = vmem((NB, FACE), F32)
     blocks = lambda n, width=FACE: vmem((n, 8, width), F32)
     scratch = dict(
@@ -501,7 +552,7 @@
         scale=vmem((8, FACE), F32),
         dirs3=vmem((NB, FACE), BF16),
         pad3=vmem((NB, FACE), BF16),
-        images2=vmem((3, 2 * STORED, FACE), BF16),
+        images2=vmem((4, 2 * STORED, FACE), BF16),
         end_plane=blocks(nx * nz),
         end_gy=blocks(ny),
         lam=field,
@@ -515,17 +566,19 @@
         q=[field] * 3,
         out=[vmem((6, FACE, FACE), F32)] * STEPS,
         halo=[vmem((6, FACE, FACE), F32)] * STEPS,
-        plane=[blocks(nx * nz, width) for width in widths],
-        part=[blocks(ny, width) for width in widths],
-        gy=[blocks(ny, width) for width in widths],
-        ring=[blocks(32, width) for width in widths],
+        plane=[blocks(nx * nz)] * STEPS,
+        part=[blocks(ny)] * STEPS,
+        gy=[blocks(ny)] * STEPS,
+        ring=[blocks(32)] * STEPS,
         share=[blocks(6)] * 6,
         shares=[blocks(6)] * 6,
         mine=[vmem((8, FACE), F32)] * 6,
-        sums=[blocks(ny)] * 3,
-        sums_y=[blocks(ny)] * 3,
-        sums_plane=[blocks(nx * nz)] * 3,
-        sums_all=[blocks(ny)] * 3,
+        sums=[blocks(ny)] * 4,
+        sums_y=[blocks(ny)] * 4,
+        sums_plane=[blocks(nx * nz)] * 4,
+        sums_all=[blocks(ny)] * 4,
+        pairs_y=[blocks(ny)] * 2,
+        pairs_plane=[blocks(nx * nz)] * 2,
         local=pltpu.SemaphoreType.DMA((len(given),)),
         sent=pltpu.SemaphoreType.DMA((64,)),
         came=pltpu.SemaphoreType.DMA((64,)),

time: 107 us -> 98.6 us (0.921)
  Pallas kernels: 103 us -> 94.9 us
    pallas_call x1, Pallas kernels: 103 us -> 94.9 us  [per_device(): pl.pallas_call(body, out_shape=[jax.ShapeDtypeStruct((NB, FACE), F32)] *...]
where the time goes in v2:
time: 98.6 us; the launch traced here: 98.5 us
  Pallas kernels  94.9 us (96%)
  other arithmetic  2.31 us (2%)
  between operations  1.29 us (1%)
    pallas_call x1, Pallas kernels, per_device(): pl.pallas_call(body, out_shape=[jax.ShapeDtypeStruct((NB, FACE), F32)] *...  94.9 us
    sub x1, other arithmetic, per_device(): res - rate * image  2.31 us

profile of v2, /device:TPU:1, one launch (start us, length us, event | category | flops | bytes accessed | tf_op | source)
XLA Modules:
  0.0 98.5 jit_solution(6405023709080604400)
XLA Ops:
  1.3 94.9 %feti.1 = (f32[768,128]{1,0:T(8,128)}, f32[768,128]{1,0:T(8,128)}, f32[768,128]{1,0:T(8,128)}, f32[768,128]{1,0:T(8,128)}, f32[1,128]{1,0:T(1,128)}) custom-call(f32[6,1,1536]{2,1,0:T(1,128)} %bitcast.24, f32[6,1,128]{2,1,0:T(1,128)} %bitcast.26, s32[1,1]{1,0:T(1,128)} %bitcast.17.refs_2_, f32[6,6,1,128]{3,2,1,0:T(1,128)} %bitcast.25, f32[768,768]{1,0:T(8,128)} %bitcast.18, ...), custom_call_target="tpu_custom_call" | custom-call | tf_op jit(solution)/shard_map/feti/pallas_call | solution.py:595
  96.2 2.3 %multiply_subtract_fusion = (f32[768,128]{1,0:T(8,128)}, f32[768,128]{1,0:T(8,128)}) fusion(f32[768,128]{1,0:T(8,128)} %get-tuple-element.10, f32[768,128]{1,0:T(8,128)} %get-tuple-element.11, f32[128]{0:T(128)} %bitcast.28, f32[768,128]{1,0:T(8,128)} %get-tuple-element.7, f32[768,128]{1,0:T(8,128)} %get-tuple-element.9), kind=kLoop, calls=%fused_computation | loop fusion | flops 393216 | bytes 2359808 | tf_op jit(solution)/shard_map/sub | solution.py:607

commit v3 on v2

--- a/solution.py
+++ b/solution.py
@@ -62,8 +62,12 @@
     def at_offset(offset):
         return {axis: other(axis, d) for axis, d in zip(AXES, offset) if d}
 
-    plane = [(dx, 0, dz) for dx in range(nx) for dz in range(nz) if dx or dz]
-    line = [(0, dy, 0) for dy in range(1, ny)]
+    def nearness(offset):
+        x, y, z = (min(d % n, -d % n) for d, n in zip(offset, sizes))
+        return -(x / 2 + y + z)
+
+    plane = sorted(((dx, 0, dz) for dx in range(nx) for dz in range(nz) if dx or dz), key=nearness)
+    line = sorted(((0, dy, 0) for dy in range(1, ny)), key=nearness)
     corner = [o for o in RING if o[1] and (o[0] or o[2])]
 
     barrier = pltpu.get_barrier_semaphore()
@@ -104,20 +108,20 @@
             send(piece(slot), dst.at[slot ^ 1], sems, at_offset(ACROSS[slot]))
         return finish(sems, dst)
 
-    def to_all(axis, value, dst):
+    def to_all(value, dst):
         sems = phase()
-        dst[me[axis]] = value
-        for delta in range(1, count[axis]):
-            send(dst.at[me[axis]], dst.at[me[axis]], sems, {axis: other(axis, delta)})
-        return finish(sems, dst.at[pl.ds(0, count[axis] - 1)])
-
-    def to_each(axis, src, dst):
+        dst[me[GY]] = value
+        for _, delta, _ in line:
+            send(dst.at[me[GY]], dst.at[me[GY]], sems, {GY: other(GY, delta)})
+        return finish(sems, dst.at[pl.ds(0, ny - 1)])
+
+    def to_each(src, dst):
         sems = phase()
-        for delta in range(1, count[axis]):
-            peer = other(axis, delta)
-            send(src.at[peer], dst.at[me[axis]], sems, {axis: peer})
-        dst[me[axis]] = src[me[axis]]
-        return finish(sems, dst.at[pl.ds(0, count[axis] - 1)])
+        for _, delta, _ in line:
+            peer = other(GY, delta)
+            send(src.at[peer], dst.at[me[GY]], sems, {GY: peer})
+        dst[me[GY]] = src[me[GY]]
+        return finish(sems, dst.at[pl.ds(0, ny - 1)])
 
     def to_plane(value, dst):
         spot = me[GZ] * nx + me[GX]
@@ -130,7 +134,7 @@
     def to_ring(value, dst, reach=len(RING)):
         dst[0] = value
         sems = phase()
-        for j in range(1, reach):
+        for j in sorted(range(1, reach), key=lambda j: nearness(RING[j])):
             send(dst.at[0], dst.at[j], sems, at_offset(tuple(-d for d in RING[j])))
         return finish(sems, dst.at[pl.ds(1, reach - 1)])
 
@@ -144,6 +148,11 @@
         high, low = split(x)
         return high.astype(F32), low.astype(F32)
 
+    def eight(x):
+        shape = list(x.shape)
+        shape[-2] = 8 - shape[-2]
+        return jnp.concatenate([x, jnp.zeros(shape, F32)], axis=x.ndim - 2)
+
     def slot_rows(slot):
         return slice(slot * FACE, (slot + 1) * FACE)
 
@@ -151,10 +160,9 @@
         return ref[slot_rows(slot), :]
 
     group = nz * 6
-    s.own_rows[...] = jnp.zeros_like(s.own_rows)
     s.cut[...] = jnp.zeros_like(s.cut)
     fetch.rows.wait()
-    s.own_rows[0:6, :] = got.rows[:, 0, :]
+    s.own_rows[...] = got.rows[:, 0, :]
     for j in range(ny):
         for i in range(nx):
             at = (i * ny + j) * group
@@ -170,66 +178,6 @@
         own_modes[slot, 0:6, :] = jnp.where(present, sign * got.traces[:, slot, 0, :], 0.0)
 
     fetch.load.wait()
-    s.block0[...] = jnp.zeros_like(s.block0)
-    s.block0[0:6, :] = got.load[:, 0, :]
-
-    pl.semaphore_wait(barrier, len(peers))
-
-    def coarse_y(k):
-        c = s.plane[k][...].reshape(nx * nz * 8, FACE)
-        s.part[k][...] = fold(dot(s.inverse[...], wide(c)), ny * 8).reshape(ny, 8, FACE)
-        return to_each(GY, s.part[k], s.gy[k])
-
-    def graph(k, slot):
-        own = s.ring[k][0]
-        near = s.ring[k][1 + slot]
-        high, low = halves(jnp.concatenate([own, near], axis=0))
-        stack = jnp.concatenate([high, high, low, jnp.zeros((FACE - 48, FACE), F32)], axis=0).astype(BF16)
-        return dot(s.basis[slot], stack)
-
-    def modes_dot(z):
-        return fold(dot(s.modes2[...], wide(z)), 8)
-
-    def apply(x):
-        return fold(dot(s.op2[...], wide(x)), NB)
-
-    def spread(r, k):
-        own = None
-        for slot in range(6):
-            part = fold(dot(s.both2[slot], wide(r[slot_rows(slot), :])), 16)
-            own = part[0:8] if own is None else own + part[0:8]
-            s.share[k][slot] = part[8:16]
-        came = to_faces(lambda slot: s.share[k].at[slot], s.shares[k])
-        s.mine[k][...] = own
-        return came
-
-    def gathered(k):
-        return s.mine[k][...] + total(s.shares[k])
-
-    def stencil(k):
-        return fold(dot(s.stencil2[...], wide(s.ring[k][...].reshape(256, FACE))), 8)
-
-    def operate(k, x, load=None):
-        out = apply(x)
-        for slot in range(6):
-            part = out[slot_rows(slot), :]
-            if load is not None:
-                part = (1.0 if slot % 2 else -1.0) * face(load, slot) - part
-            s.out[k][slot] = part
-        return to_faces(lambda slot: s.out[k].at[slot], s.halo[k])
-
-    def assembled(k):
-        return (s.out[k][...] + s.halo[k][...]).reshape(NB, FACE)
-
-    came_cut = to_each(GY, s.cut, s.all_cut)
-    came_plane = to_plane(s.block0[...], s.plane[0])
-    came_modes = to_faces(lambda slot: own_modes.at[slot], s.near_modes)
-
-    modes = jnp.concatenate([own_modes[slot] for slot in range(6)], axis=1)
-    s.modes2[...] = jnp.concatenate(halves(modes), axis=0).astype(BF16)
-    for k in (0, 1, 2, 3, STORED_STEP):
-        tail = s.ring[k].shape
-        s.ring[k][len(RING) :] = jnp.zeros((tail[0] - len(RING), *tail[1:]), F32)
 
     fetch.flex.wait()
     fetch.bmap.wait()
@@ -244,6 +192,68 @@
         s.pick[at, :] = jnp.where(got.bmap[...] == spot, sign, 0.0).astype(BF16)
         return carry
 
+    lax.fori_loop(0, 6, cut_flex, 0)
+
+    pl.semaphore_wait(barrier, len(peers))
+
+    def coarse_y(k):
+        c = eight(s.plane[k][...]).reshape(nx * nz * 8, FACE)
+        part = fold(dot(s.inverse[...], wide(c)), ny * 8).reshape(ny, 8, FACE)
+        for j in range(ny):
+            s.part[k][j] = part[j, 0:6]
+        return to_each(s.part[k], s.gy[k])
+
+    def graph(k, slot):
+        own = eight(s.ring[k][0])
+        near = eight(s.ring[k][1 + slot])
+        high, low = halves(jnp.concatenate([own, near], axis=0))
+        stack = jnp.concatenate([high, high, low, jnp.zeros((FACE - 48, FACE), F32)], axis=0).astype(BF16)
+        return dot(s.basis[slot], stack)
+
+    def modes_dot(z):
+        return fold(dot(s.modes2[...], wide(z)), 8)[0:6]
+
+    def apply(x):
+        return fold(dot(s.op2[...], wide(x)), NB)
+
+    def spread(r, k):
+        own = None
+        for slot in range(6):
+            part = fold(dot(s.both2[slot], wide(r[slot_rows(slot), :])), 16)
+            own = part[0:6] if own is None else own + part[0:6]
+            s.share[k][slot] = part[8:14]
+        came = to_faces(lambda slot: s.share[k].at[slot], s.shares[k])
+        s.mine[k][...] = own
+        return came
+
+    def gathered(k):
+        return s.mine[k][...] + total(s.shares[k])
+
+    def stencil(k):
+        return fold(dot(s.stencil2[...], wide(eight(s.ring[k][...]).reshape(256, FACE))), 8)[0:6]
+
+    def operate(k, x, load=None):
+        out = apply(x)
+        for slot in range(6):
+            part = out[slot_rows(slot), :]
+            if load is not None:
+                part = (1.0 if slot % 2 else -1.0) * face(load, slot) - part
+            s.out[k][slot] = part
+        return to_faces(lambda slot: s.out[k].at[slot], s.halo[k])
+
+    def assembled(k):
+        return (s.out[k][...] + s.halo[k][...]).reshape(NB, FACE)
+
+    came_cut = to_each(s.cut, s.all_cut)
+    came_plane = to_plane(got.load[:, 0, :], s.plane[0])
+    came_modes = to_faces(lambda slot: own_modes.at[slot], s.near_modes)
+
+    modes = jnp.concatenate([own_modes[slot] for slot in range(6)], axis=1)
+    s.modes2[...] = jnp.concatenate(halves(modes), axis=0).astype(BF16)
+    for k in (0, 1, 2, 3, STORED_STEP):
+        tail = s.ring[k].shape
+        s.ring[k][len(RING) :] = jnp.zeros((tail[0] - len(RING), *tail[1:]), F32)
+
     def pick_rows(i, carry):
         at = pl.multiple_of(i * FACE, FACE)
         out = dot(s.pick[pl.ds(at, FACE), :], s.flex2[...])
@@ -257,12 +267,11 @@
         s.op2[at, :] = out.astype(BF16)
         return carry
 
-    lax.fori_loop(0, 6, cut_flex, 0)
     lax.fori_loop(0, 6, pick_rows, 0)
-    lax.fori_loop(0, 6, pick_columns, 0)
+    lax.fori_loop(0, 3, pick_columns, 0)
 
     came_cut()
-    wide_cut = s.all_cut[...].reshape(ny * 8, s.all_cut.shape[-1])
+    wide_cut = eight(s.all_cut[...]).reshape(ny * 8, s.all_cut.shape[-1])
     col = lax.broadcasted_iota(jnp.int32, (256, 256), 1)
     row = lax.broadcasted_iota(jnp.int32, (256, 256), 0)
     place = lax.rem(lax.div(col, 8), nx) * group + lax.div(col, 8 * nx) * 6 + lax.rem(col, 8)
@@ -272,6 +281,7 @@
     came_plane()
     came_y = coarse_y(0)
 
+    lax.fori_loop(3, 6, pick_columns, 0)
     came_modes()
     for slot in range(6):
         own, near = own_modes[slot], s.near_modes[slot]
@@ -293,7 +303,7 @@
     lane = lax.broadcasted_iota(jnp.int32, (8, FACE), 1)
     parts = [jnp.zeros((8, FACE), F32)] * 2
     for j, base in enumerate((ZERO, *ACROSS)):
-        source = s.mine[0][...] if j == 0 else s.shares[0][j - 1]
+        source = eight(s.mine[0][...] if j == 0 else s.shares[0][j - 1])
         for b, step in enumerate((ZERO, *ACROSS)):
             to = RING.index(plus(base, step))
             moved = pltpu.roll(source, (8 * (to % 16) - 8 * b) % FACE, 1)
@@ -345,14 +355,15 @@
         def __init__(self, j, field, alpha):
             self.j = j
             parts = [field[slot_rows(slot), :] for slot in (1, 3, 5)]
-            parts.append(jnp.concatenate([-alpha, jnp.zeros((FACE - 8, FACE), F32)], axis=0))
+            parts.append(jnp.concatenate([eight(-alpha), jnp.zeros((FACE - 8, FACE), F32)], axis=0))
             out = None
             for i, part in enumerate(parts):
                 term = dot(s.images2[i], wide(part))
                 out = term if out is None else out + term
-            flat = jnp.concatenate([fold(out, STORED), jnp.zeros((64 - STORED, FACE), F32)], axis=0)
-            s.sums[j][...] = flat.reshape(8, 8, FACE)
-            self.came = to_each(GY, s.sums[j], s.sums_y[j])
+            flat, cut = fold(out, STORED), STORED // ny
+            for i in range(ny):
+                s.sums[j][i] = flat[i * cut : (i + 1) * cut]
+            self.came = to_each(s.sums[j], s.sums_y[j])
 
         def share(self):
             self.came()
@@ -360,11 +371,11 @@
 
         def collect(self):
             self.came()
-            self.came = to_all(GY, total(s.sums_plane[self.j]), s.sums_all[self.j])
+            self.came = to_all(total(s.sums_plane[self.j]), s.sums_all[self.j])
 
         def result(self):
             self.came()
-            return s.sums_all[self.j][...].reshape(64, FACE)[0:STORED]
+            return jnp.concatenate([s.sums_all[self.j][i] for i in range(ny)], axis=0)
 
     came_y()
     alpha = total(s.gy[1])
@@ -389,16 +400,18 @@
         came_pairs, came_d, came_share, sums_d, sums_z = None, None, None, None, None
         if pairs:
             lines = [odd_dot(a, b) for a, b in pairs]
-            lines.append(jnp.zeros((8 - len(lines), FACE), F32))
-            came_pairs = to_all(GY, jnp.concatenate(lines, axis=0), s.pairs_y[j])
+            came_pairs = to_all(jnp.concatenate(lines, axis=0), s.pairs_y[j])
         sums[0].share()
         came_halo = operate(k, v[...])
         if k == 2:
             came_plane_d()
             came_y_d = coarse_y(STORED_STEP)
+        if k == 4:
+            came_pairs()
+            came_pairs = to_plane(total(s.pairs_y[j]), s.pairs_plane[j])
         came_plane()
         came_y = coarse_y(k)
-        if pairs:
+        if k == 3:
             came_pairs()
             came_pairs = to_plane(total(s.pairs_y[j]), s.pairs_plane[j])
         for each in sums:
@@ -433,10 +446,10 @@
 
     p, q = s.p, s.q
     came_ring, _, later = superstep(2, w, (), came_plane, [sums_w])
-    modes_pad3 = thrice(gathered(3) - stencil(STORED_STEP))
+    modes_pad3 = thrice(eight(gathered(3) - stencil(STORED_STEP)))
     gram = sums_w.result()
     stack = stored_part(gram)
-    modes_off = gathered(4) - dot(modes_pad3, stack)
+    modes_off = gathered(4) - dot(modes_pad3, stack)[0:6]
     came_ring()
     change = stencil(2)
     modes_q = modes_off - change
@@ -472,7 +485,7 @@
         gram = gram - rate * gram_q
         stack = stored_part(gram)
         if k == 0:
-            modes_off = modes_paw - rate * gathered(5) - dot(modes_pad3, stack) - gammas[0] * modes_q
+            modes_off = modes_paw - rate * gathered(5) - dot(modes_pad3, stack)[0:6] - gammas[0] * modes_q
         w[...] = w[...] - rate * q[k][...]
         new = w[...] - dot(s.dirs3[...], stack)
         off = dot(s.pad3[...], stack)
@@ -496,7 +509,7 @@
     for slot in (1, 3, 5):
         known = face(q[2], slot) - rate * face(z, slot)
         over = over + jnp.sum(face(p[2], slot) * known, axis=0, keepdims=True)
-    lines = jnp.concatenate([over, odd_dot(p[2], w), jnp.zeros((6, FACE), F32)], axis=0)
+    lines = jnp.concatenate([over, odd_dot(p[2], w)], axis=0)
     came_end = to_plane(lines, s.end_plane)
     came_ring()
     for slot in range(6):
@@ -507,7 +520,7 @@
     dir_out[...] = p[2][...]
     res_out[...] = w[...]
     came_end()
-    to_all(GY, total(s.end_plane), s.end_gy)()
+    to_all(total(s.end_plane), s.end_gy)()
     lines = total(s.end_gy)
     rate_out[...] = lines[1:2] / lines[0:1]
 
@@ -531,30 +544,29 @@
         images=images.reshape(STORED, 6, FACE).swapaxes(0, 1),
     )
     field = vmem((NB, FACE), F32)
-    blocks = lambda n, width=FACE: vmem((n, 8, width), F32)
+    blocks = lambda n, width=FACE, rows=6: vmem((n, rows, width), F32)
     scratch = dict(
         given={name: vmem(x.shape, x.dtype) for name, x in given.items()},
         flex2=vmem((NB, 2 * NB), BF16),
         pick=vmem((NB, NB), BF16),
         half=vmem((2 * NB, NB), BF16),
         op2=vmem((2 * NB, NB), BF16),
-        own_rows=vmem((8, 6 * nx * ny * nz), F32),
+        own_rows=vmem((6, 6 * nx * ny * nz), F32),
         cut=blocks(ny, 256),
         all_cut=blocks(ny, 256),
         inverse=vmem((2 * ny * 8, nx * nz * 8), BF16),
-        own_modes=blocks(6),
-        near_modes=blocks(6),
+        own_modes=blocks(6, rows=8),
+        near_modes=blocks(6, rows=8),
         modes2=vmem((16, NB), BF16),
         both2=vmem((6, 32, FACE), BF16),
         stencil2=vmem((16, 256), BF16),
         basis=vmem((6, FACE, FACE), BF16),
-        block0=vmem((8, FACE), F32),
         scale=vmem((8, FACE), F32),
         dirs3=vmem((NB, FACE), BF16),
         pad3=vmem((NB, FACE), BF16),
         images2=vmem((4, 2 * STORED, FACE), BF16),
-        end_plane=blocks(nx * nz),
-        end_gy=blocks(ny),
+        end_plane=blocks(nx * nz, rows=2),
+        end_gy=blocks(ny, rows=2),
         lam=field,
         w=field,
         z=field,
@@ -572,13 +584,13 @@
         ring=[blocks(32)] * STEPS,
         share=[blocks(6)] * 6,
         shares=[blocks(6)] * 6,
-        mine=[vmem((8, FACE), F32)] * 6,
-        sums=[blocks(ny)] * 4,
-        sums_y=[blocks(ny)] * 4,
-        sums_plane=[blocks(nx * nz)] * 4,
-        sums_all=[blocks(ny)] * 4,
-        pairs_y=[blocks(ny)] * 2,
-        pairs_plane=[blocks(nx * nz)] * 2,
+        mine=[vmem((6, FACE), F32)] * 6,
+        sums=[blocks(ny, rows=STORED // ny)] * 4,
+        sums_y=[blocks(ny, rows=STORED // ny)] * 4,
+        sums_plane=[blocks(nx * nz, rows=STORED // ny)] * 4,
+        sums_all=[blocks(ny, rows=STORED // ny)] * 4,
+        pairs_y=[blocks(ny, rows=4 + k) for k in range(2)],
+        pairs_plane=[blocks(nx * nz, rows=4 + k) for k in range(2)],
         local=pltpu.SemaphoreType.DMA((len(given),)),
         sent=pltpu.SemaphoreType.DMA((64,)),
         came=pltpu.SemaphoreType.DMA((64,)),
@@ -594,7 +606,7 @@
     outside = pl.BlockSpec(memory_space=pltpu.HBM)
     lam, direction, res, image, rate = pl.pallas_call(
         body,
-        out_shape=[jax.ShapeDtypeStruct((NB, FACE), F32)] * 4 + [jax.ShapeDtypeStruct((1, FACE), F32)],
+        out_shape=[vmem((NB, FACE), F32)] * 4 + [vmem((1, FACE), F32)],
         in_specs=[outside] * len(given),
         out_specs=[inside] * 5,
         scratch_shapes=leaves,

time: 98.6 us -> 89.3 us (0.906)
  Pallas kernels: 94.9 us -> 86.9 us
  other arithmetic: 2.31 us -> 0.96 us
    pallas_call x1, Pallas kernels: 94.9 us -> 86.9 us  [per_device(): pl.pallas_call(body, out_shape=[vmem((NB, FACE), F32)] * 4 + [vmem((1, FA...]
    sub x1, other arithmetic: 2.31 us -> 0.96 us  [per_device(): res - rate * image]
where the time goes in v3:
time: 89.3 us; the launch traced here: 89.1 us
  Pallas kernels  86.9 us (97%)
  between operations  1.29 us (1%)
  other arithmetic  0.96 us (1%)
    pallas_call x1, Pallas kernels, per_device(): pl.pallas_call(body, out_shape=[vmem((NB, FACE), F32)] * 4 + [vmem((1, FA...  86.9 us

profile of v3, /device:TPU:1, one launch (start us, length us, event | category | flops | bytes accessed | tf_op | source)
XLA Modules:
  0.0 89.1 jit_solution(13671032389935415707)
XLA Ops:
  1.3 86.9 %feti.1 = (f32[768,128]{1,0:T(8,128)S(1)}, f32[768,128]{1,0:T(8,128)S(1)}, f32[768,128]{1,0:T(8,128)S(1)}, f32[768,128]{1,0:T(8,128)S(1)}, f32[1,128]{1,0:T(1,128)S(1)}) custom-call(f32[6,1,1536]{2,1,0:T(1,128)} %bitcast.25, f32[6,1,128]{2,1,0:T(1,128)} %bitcast.27, s32[1,1]{1,0:T(1,128)} %bitcast.17.refs_2_, f32[6,6,1,128]{3,2,1,0:T(1,128)} %bitcast.26, ...), custom_call_target="tpu_custom_call" | custom-call | tf_op jit(solution)/shard_map/feti/pallas_call | solution.py:607
  88.2 1.0 %multiply_subtract_fusion = (f32[768,128]{1,0:T(8,128)}, f32[768,128]{1,0:T(8,128)}) fusion(f32[768,128]{1,0:T(8,128)S(1)} %get-tuple-element.10, f32[768,128]{1,0:T(8,128)S(1)} %get-tuple-element.11, f32[128]{0:T(128)S(1)} %bitcast.18, f32[768,128]{1,0:T(8,128)S(1)} %get-tuple-element.7, f32[768,128]{1,0:T(8,128)S(1)} %get-tuple-element.9), kind=kLoop, calls=%fused_computation | loop fusion | flops 393216 | bytes 2359808 | tf_op jit(solution)/shard_map/sub | solution.py:619

commit v4 on v3

--- a/solution.py
+++ b/solution.py
@@ -15,6 +15,7 @@
 STORED = 40
 STEPS = 6
 STORED_STEP = 5
+ODD_FIRST = (1, 3, 5, 0, 2, 4)
 ACROSS = tuple(tuple((1 if slot % 2 else -1) if axis == slot // 2 else 0 for axis in range(3)) for slot in range(6))
 ZERO = (0, 0, 0)
 
@@ -192,6 +193,13 @@
         s.pick[at, :] = jnp.where(got.bmap[...] == spot, sign, 0.0).astype(BF16)
         return carry
 
+    def pick_rows(i, carry):
+        at = pl.multiple_of(i * 2 * FACE, 2 * FACE)
+        out = dot(s.pick[pl.ds(at, 2 * FACE), :], s.flex2[...])
+        s.half[pl.ds(at, 2 * FACE), :] = out[:, 0:NB].astype(BF16)
+        s.half[pl.ds(NB + at, 2 * FACE), :] = out[:, NB : 2 * NB].astype(BF16)
+        return carry
+
     lax.fori_loop(0, 6, cut_flex, 0)
 
     pl.semaphore_wait(barrier, len(peers))
@@ -254,21 +262,14 @@
         tail = s.ring[k].shape
         s.ring[k][len(RING) :] = jnp.zeros((tail[0] - len(RING), *tail[1:]), F32)
 
-    def pick_rows(i, carry):
-        at = pl.multiple_of(i * FACE, FACE)
-        out = dot(s.pick[pl.ds(at, FACE), :], s.flex2[...])
-        s.half[pl.ds(at, FACE), :] = out[:, 0:NB].astype(BF16)
-        s.half[pl.ds(NB + at, FACE), :] = out[:, NB : 2 * NB].astype(BF16)
-        return carry
-
     def pick_columns(i, carry):
-        at = pl.ds(pl.multiple_of(i * 2 * FACE, 2 * FACE), 2 * FACE)
+        at = pl.ds(pl.multiple_of(i * 4 * FACE, 4 * FACE), 4 * FACE)
         out = lax.dot_general(s.half[at, :], s.pick[...], (((1,), (1,)), ((), ())), preferred_element_type=F32)
         s.op2[at, :] = out.astype(BF16)
         return carry
 
-    lax.fori_loop(0, 6, pick_rows, 0)
-    lax.fori_loop(0, 3, pick_columns, 0)
+    lax.fori_loop(0, 3, pick_rows, 0)
+    lax.fori_loop(0, 2, pick_columns, 0)
 
     came_cut()
     wide_cut = eight(s.all_cut[...]).reshape(ny * 8, s.all_cut.shape[-1])
@@ -281,7 +282,7 @@
     came_plane()
     came_y = coarse_y(0)
 
-    lax.fori_loop(3, 6, pick_columns, 0)
+    lax.fori_loop(2, 3, pick_columns, 0)
     came_modes()
     for slot in range(6):
         own, near = own_modes[slot], s.near_modes[slot]
@@ -394,6 +395,8 @@
             part = jnp.sum(face(a, slot) * face(b, slot), axis=0, keepdims=True)
             out = part if out is None else out + part
         return out
+
+    modes_made = []
 
     def superstep(k, v, pairs, came_plane, sums):
         j = k - 3
@@ -427,6 +430,9 @@
             sums_d = StoredSums(1, zd[...], alpha)
         if k < 4:
             came_share = spread(apply(z[...]), k + 2)
+        else:
+            modes_made.extend(modes_dot(x[...]) for x in (w, s.q[1], s.p[0], s.p[1]))
+            modes_made.append(thrice(eight(modes_dot(s.field_d[...]))))
         came_y()
         alpha = total(s.gy[k])
         came_ring = to_ring(alpha, s.ring[k], len(RING) if k < 4 else 7)
@@ -461,6 +467,17 @@
         s.pad3[at, :] = thrice(face(zd, slot) - graph(STORED_STEP, slot))
     q[0][...] = paw[...] - dot(s.pad3[...], stack)
     p[0][...] = w[...] - dot(s.dirs3[...], stack)
+
+    def step(slot, rate, gammas, stack):
+        at = slot_rows(slot)
+        w[at, :] = w[at, :] - rate * q[1][at, :]
+        new = w[at, :] - dot(s.dirs3[at, :], stack)
+        off = dot(s.pad3[at, :], stack)
+        for j in range(2):
+            new = new - p[j][at, :] * gammas[j]
+            off = off + q[j][at, :] * gammas[j]
+        p[2][at, :] = new
+        q[2][at, :] = paw[at, :] - off - rate * z[at, :]
 
     own, curves = [], []
     for k in range(2):
@@ -486,35 +503,34 @@
         stack = stored_part(gram)
         if k == 0:
             modes_off = modes_paw - rate * gathered(5) - dot(modes_pad3, stack)[0:6] - gammas[0] * modes_q
-        w[...] = w[...] - rate * q[k][...]
-        new = w[...] - dot(s.dirs3[...], stack)
-        off = dot(s.pad3[...], stack)
-        for j in range(k + 1):
-            new = new - p[j][...] * gammas[j]
-            off = off + q[j][...] * gammas[j]
-        p[k + 1][...] = new
-        lam[...] = lam[...] + rate * p[k][...]
-        if k == 0:
-            q[1][...] = paw[...] - rate * z[...] - off
-            came_ring()
-            came_plane = to_plane(modes_off + rate * stencil(3), s.plane[4])
-            for slot in range(6):
-                at = slot_rows(slot)
-                change = rate * graph(3, slot)
-                paw[at, :] = paw[at, :] - rate * face(z, slot) + change
-                q[1][at, :] = q[1][at, :] + change
-
-    over = rate * jnp.sum(modes_dot(p[2][...]) * s.ring[4][0], axis=0, keepdims=True)
-    q[2][...] = paw[...] - off
-    for slot in (1, 3, 5):
-        known = face(q[2], slot) - rate * face(z, slot)
-        over = over + jnp.sum(face(p[2], slot) * known, axis=0, keepdims=True)
-    lines = jnp.concatenate([over, odd_dot(p[2], w)], axis=0)
+        if k == 1:
+            break
+        w[...] = w[...] - rate * q[0][...]
+        p[1][...] = w[...] - dot(s.dirs3[...], stack) - p[0][...] * gammas[0]
+        q[1][...] = paw[...] - rate * z[...] - dot(s.pad3[...], stack) - q[0][...] * gammas[0]
+        lam[...] = lam[...] + rate * p[0][...]
+        came_ring()
+        came_plane = to_plane(modes_off + rate * stencil(3), s.plane[4])
+        for slot in ODD_FIRST:
+            at = slot_rows(slot)
+            change = rate * graph(3, slot)
+            paw[at, :] = paw[at, :] - rate * face(z, slot) + change
+            q[1][at, :] = q[1][at, :] + change
+
+    modes_p = modes_made[0] - rate * modes_made[1] - gammas[0] * modes_made[2] - gammas[1] * modes_made[3]
+    modes_p = modes_p - dot(modes_made[4], stack)[0:6]
+    over = rate * jnp.sum(modes_p * s.ring[4][0], axis=0, keepdims=True)
+    for slot in ODD_FIRST[:3]:
+        step(slot, rate, gammas, stack)
+    lines = jnp.concatenate([over + odd_dot(p[2], q[2]), odd_dot(p[2], w)], axis=0)
     came_end = to_plane(lines, s.end_plane)
+    for slot in ODD_FIRST[3:]:
+        step(slot, rate, gammas, stack)
+    lam[...] = lam[...] + rate * p[1][...]
     came_ring()
     for slot in range(6):
         at = slot_rows(slot)
-        image_out[at, :] = q[2][at, :] - rate * (face(z, slot) - graph(4, slot))
+        image_out[at, :] = q[2][at, :] + rate * graph(4, slot)
 
     lam_out[...] = lam[...]
     dir_out[...] = p[2][...]

time: 89.3 us -> 88.9 us (level)
  no operation moved by 1% of the time
where the time goes in v4:
time: 88.9 us; the launch traced here: 88.8 us
  Pallas kernels  86.5 us (97%)
  between operations  1.29 us (1%)
  other arithmetic  0.96 us (1%)
    pallas_call x1, Pallas kernels, per_device(): pl.pallas_call(body, out_shape=[vmem((NB, FACE), F32)] * 4 + [vmem((1, FA...  86.5 us

profile of v4, /device:TPU:1, one launch (start us, length us, event | category | flops | bytes accessed | tf_op | source)
XLA Modules:
  0.0 88.8 jit_solution(8121654565851609253)
XLA Ops:
  1.3 86.5 %feti.1 = (f32[768,128]{1,0:T(8,128)S(1)}, f32[768,128]{1,0:T(8,128)S(1)}, f32[768,128]{1,0:T(8,128)S(1)}, f32[768,128]{1,0:T(8,128)S(1)}, f32[1,128]{1,0:T(1,128)S(1)}) custom-call(f32[6,1,1536]{2,1,0:T(1,128)} %bitcast.25, f32[6,1,128]{2,1,0:T(1,128)} %bitcast.27, s32[1,1]{1,0:T(1,128)} %bitcast.17.refs_2_, f32[6,6,1,128]{3,2,1,0:T(1,128)} %bitcast.26, ...), custom_call_target="tpu_custom_call" | custom-call | tf_op jit(solution)/shard_map/feti/pallas_call | solution.py:623
  87.8 1.0 %multiply_subtract_fusion = (f32[768,128]{1,0:T(8,128)}, f32[768,128]{1,0:T(8,128)}) fusion(f32[768,128]{1,0:T(8,128)S(1)} %get-tuple-element.10, f32[768,128]{1,0:T(8,128)S(1)} %get-tuple-element.11, f32[128]{0:T(128)S(1)} %bitcast.18, f32[768,128]{1,0:T(8,128)S(1)} %get-tuple-element.7, f32[768,128]{1,0:T(8,128)S(1)} %get-tuple-element.9), kind=kLoop, calls=%fused_computation | loop fusion | flops 393216 | bytes 2359808 | tf_op jit(solution)/shard_map/sub | solution.py:635
